TPU v7x, 32 devices: a whole 2x2x4 slice. The times are simulated.
32 devices in a mesh: dp: 2 (over x), row: 4 (over y, core), col: 4 (over z).
Axes of the slice: x: 2, y: 2, z: 4, core: 2. Of those that a mesh axis runs over, the one named last changes fastest.
Arguments:
- latents: float32 [24, 32, 128], P(('dp', 'row')), may hold values from -6 to 6
- labels: int32 [24], P(('dp', 'row')), may hold values from 0 to 999
- step_index: int32 [24], P(('dp', 'row')), may hold values from 1 to 8
- seeds: int32 [24], P(('dp', 'row')), may hold values from 0 to 2147483646
- class_table: bfloat16 [1000, 1152], replicated, may hold values from -6 to 6
- teacher_patch: bfloat16 [16, 1152], replicated, may hold values from -1.5 to 1.5
- teacher_mod: bfloat16 [1152, 3, 1152], P(('dp', 'row'), None, 'col'), may hold values from -0.1875 to 0.1875
- teacher_up: bfloat16 [1152, 4608], P(('dp', 'row'), 'col'), may hold values from -0.1875 to 0.1875
- teacher_down: bfloat16 [1152, 4608], P(('dp', 'row'), 'col'), may hold values from -0.09375 to 0.09375
- teacher_out: bfloat16 [16, 1152], replicated, may hold values from -0.1875 to 0.1875
- student_patch: bfloat16 [16, 1152], replicated, may hold values from -1.5 to 1.5
- student_mod: bfloat16 [1152, 3, 1152], P(('dp', 'row'), None, 'col'), may hold values from -0.1875 to 0.1875
- student_up: bfloat16 [1152, 4608], P(('dp', 'row'), 'col'), may hold values from -0.1875 to 0.1875
- student_down: bfloat16 [1152, 4608], P(('dp', 'row'), 'col'), may hold values from -0.09375 to 0.09375
- student_out: bfloat16 [16, 1152], replicated, may hold values from -0.1875 to 0.1875
Outputs:
- up_gradient: float32 [1152, 4608], P(('dp', 'row'), 'col')
- down_gradient: float32 [1152, 4608], P(('dp', 'row'), 'col')
All inputs are finite; a program needn't handle non-finite values.
Results may differ from a plain program's by a relative error of at most 0.002.
Values may be sent and summed in bfloat16 or wider, within the bound.
No kernel may reach another device: no remote copies, remote signals or barrier semaphores. Data moves between devices by JAX's collectives and lax.ppermute only.
A program may use at most 128 MiB of HBM per device.

v0:
```python
import functools
import math

import jax
import jax.numpy as jnp
from jax import lax
from jax.experimental import pallas as pl
from jax.experimental.pallas import tpu as pltpu
from jax.sharding import PartitionSpec as P


D = 1152
CLASSES = 1000
SEQ = 256
PATCH = 16
STEPS = 8

HALF_PI = 0.5 * math.pi
ROOT_TWO_PI = math.sqrt(2.0 / math.pi)
PLANE = ("dp", "row")
F32 = jnp.float32
BF16 = jnp.bfloat16
VMEM_LIMIT = 30 * 1024 * 1024


def plan(times):
    return (jnp.cos(HALF_PI * times), jnp.sin(HALF_PI * times))


def mixing(value):
    amount = jnp.int32(16)
    value = value ^ lax.shift_right_logical(value, amount)
    value = value * 73244475
    value = value ^ lax.shift_right_logical(value, amount)
    value = value * 73244475
    value = value ^ lax.shift_right_logical(value, amount)
    return value


def noise_at(seeds, places):
    mixed = mixing(seeds * 1103515245 + places * 40503 + 12345)
    uniform = (lax.shift_right_logical(mixed, jnp.int32(8)).astype(F32) + 0.5) * (1.0 / 16777216.0)
    return math.sqrt(2.0) * lax.erf_inv(2.0 * uniform - 1.0)


def column_tile(width, most=1152):
    best = 128
    for tile in range(128, most + 1, 128):
        if width % tile == 0:
            best = tile
    return best


def gelu(pre):
    inner = ROOT_TWO_PI * (pre + 0.044715 * (pre * pre * pre))
    return pre * (0.5 * (1.0 + jnp.tanh(inner)))


def gelu_slope(pre):
    inner = ROOT_TWO_PI * (pre + 0.044715 * pre * pre * pre)
    tangent = jnp.tanh(inner)
    return 0.5 * (1.0 + tangent) + 0.5 * pre * (1.0 - tangent * tangent) * ROOT_TWO_PI * (
        1.0 + 3.0 * 0.044715 * pre * pre
    )


def layer_norm(values):
    center = values - jnp.mean(values, axis=-1, keepdims=True)
    spread = jnp.mean(center * center, axis=-1, keepdims=True)
    reciprocal = lax.rsqrt(spread + 1e-06)
    return (center * reciprocal, reciprocal)


def dot(left, right, dims):
    return lax.dot_general(left, right, (dims, ((), ())), preferred_element_type=F32)


def upright(values):
    tokens = values.shape[1]
    eye = (
        lax.broadcasted_iota(jnp.int32, (tokens, tokens), 0)
        == lax.broadcasted_iota(jnp.int32, (tokens, tokens), 1)
    ).astype(F32).astype(BF16)
    return dot(eye, values.astype(BF16), ((1,), (1,))).astype(BF16)


def place(base, down, across):
    side = across.shape[0]
    parts = []
    for row in range(base.shape[0] // side):
        parts.append(base[row * side : (row + 1) * side] + (down[row : row + 1] + across))
    return jnp.concatenate(parts, axis=0)


def load_pieces(order, pieces, panel, sem):
    copies = []
    for spot, piece in enumerate(pieces):
        rows = piece.shape[0]
        start = pl.multiple_of(order[spot], 16) if len(pieces) > 1 else 0
        copies.append(pltpu.make_async_copy(piece, panel.at[pl.ds(start, rows), :], sem.at[spot]))
    for copy in copies:
        copy.start()
    return copies


def forward_kernel(pieces, first_mod, save, per_set, *refs):
    order, state, patch, down_pos, across, mods = refs[:6]
    refs = refs[6:]
    up_pieces, down_pieces, refs = refs[:pieces], refs[pieces : 2 * pieces], refs[2 * pieces :]
    groups, samples, _, tokens = state.shape
    outs, refs = refs[:groups], refs[groups:]
    if save:
        act, pre_out, hidden = refs[:3]
        refs = refs[3:]
        up, down, up_sem, down_sem = refs
    else:
        act, hidden, up, down, up_sem, down_sem = refs
    up_copies = load_pieces(order, up_pieces, up, up_sem)
    down_copies = load_pieces(order, down_pieces, down, down_sem)

    def embed(group, carry):
        for sample in range(samples):
            base = dot(upright(state[group, sample]), patch[...], ((1,), (0,)))
            base = place(base, down_pos[group], across[...])
            normed, _ = layer_norm(base)
            spot = (group // per_set) * samples + sample if per_set else sample
            shift = mods[spot, pl.ds(first_mod, 1), :]
            scale = mods[spot, pl.ds(first_mod + 1, 1), :]
            row = pl.multiple_of((group * samples + sample) * tokens, tokens)
            act[pl.ds(row, tokens), :] = (normed * (1.0 + scale) + shift).astype(BF16)
        return carry

    lax.fori_loop(0, groups, embed, 0)
    for copy in up_copies:
        copy.wait()
    block = samples * tokens
    halves = 2 if groups % 2 == 0 else 1
    tall = groups // halves * block

    def first(step, carry):
        at = pl.multiple_of(step * tall, tall)
        pre = dot(act[pl.ds(at, tall), :], up[...], ((1,), (0,)))
        if save:
            pre_out[pl.ds(at, tall), :] = pre
        hidden[pl.ds(at, tall), :] = gelu(pre).astype(BF16)
        return carry

    lax.fori_loop(0, halves, first, 0)
    for copy in down_copies:
        copy.wait()
    part = dot(hidden[...], down[...], ((1,), (1,))).astype(BF16)
    for group in range(groups):
        outs[group][...] = part[group * block : (group + 1) * block]


def full(memory_space=pltpu.VMEM):
    return pl.BlockSpec(memory_space=memory_space)


def forward(order, state, patch, pos, mods, up_pieces, down_pieces, first_mod, save, per_set=0):
    groups, samples, _, tokens = state.shape
    count = len(up_pieces)
    total = groups * samples * tokens
    features = patch.shape[1]
    width = up_pieces[0].shape[1]
    out_shape = [jax.ShapeDtypeStruct((samples * tokens, features), BF16)] * groups
    scratch = [
        pltpu.VMEM((features, width), BF16),
        pltpu.VMEM((features, width), BF16),
        pltpu.SemaphoreType.DMA((count,)),
        pltpu.SemaphoreType.DMA((count,)),
    ]
    if save:
        out_shape = out_shape + [
            jax.ShapeDtypeStruct((total, features), BF16),
            jax.ShapeDtypeStruct((total, width), F32),
            jax.ShapeDtypeStruct((total, width), BF16),
        ]
    else:
        scratch = [pltpu.VMEM((total, features), BF16), pltpu.VMEM((total, width), BF16)] + scratch
    return pl.pallas_call(
        functools.partial(forward_kernel, count, first_mod, save, per_set),
        out_shape=out_shape,
        in_specs=[full(pltpu.SMEM)] + [full()] * 5 + [full(pltpu.HBM)] * (2 * count),
        out_specs=[full()] * len(out_shape),
        scratch_shapes=scratch,
        compiler_params=pltpu.CompilerParams(vmem_limit_bytes=VMEM_LIMIT),
        cost_estimate=pl.CostEstimate(
            flops=4 * total * features * width, bytes_accessed=8 * features * width, transcendentals=total * width
        ),
    )(order, state, patch, *pos, mods, *up_pieces, *down_pieces)


def settle(parts, state, patch, down_pos, across, mods, out, gate_at, sample):
    tokens = state.shape[2]
    rows = slice(sample * tokens, (sample + 1) * tokens)
    mixed = parts[0][rows].astype(F32)
    for part in parts[1:]:
        mixed = mixed + part[rows].astype(F32)
    gate = mods[sample, gate_at : gate_at + 1, :]
    base = dot(upright(state[sample]), patch[...], ((1,), (0,)))
    base = place(base, down_pos[0], across[...])
    final, reciprocal = layer_norm(base + gate * mixed)
    velocity = dot(out[...], final.astype(BF16), ((1,), (1,)))
    return velocity, final, reciprocal, gate


def middle_kernel(groups, *refs):
    coefs, state, patch, down_pos, across, mods, out = refs[:7]
    parts, halfway = refs[7 : 7 + groups], refs[7 + groups]
    for sample in range(state.shape[0]):
        velocity, _, _, _ = settle(parts, state, patch, down_pos, across, mods, out, 2, sample)
        noisy = state[sample]
        alpha, sigma = coefs[sample, 0], coefs[sample, 1]
        alpha_mid, sigma_mid = coefs[sample, 2], coefs[sample, 3]
        first_x = alpha * noisy - sigma * velocity
        halfway[sample] = alpha_mid * first_x + sigma_mid * (noisy - alpha * first_x) / sigma


def middle(coefs, state, patch, pos, mods, out, parts):
    groups = len(parts)
    return pl.pallas_call(
        functools.partial(middle_kernel, groups),
        out_shape=jax.ShapeDtypeStruct(state.shape, F32),
        in_specs=[full(pltpu.SMEM)] + [full()] * (6 + groups),
        out_specs=full(),
        compiler_params=pltpu.CompilerParams(vmem_limit_bytes=VMEM_LIMIT),
        cost_estimate=pl.CostEstimate(flops=10**9, bytes_accessed=2 * 10**6, transcendentals=0),
        name="middle",
    )(coefs, state, patch, *pos, mods, out, *parts)


def last_kernel(groups, *refs):
    coefs, noisy_ref, half_ref, t_patch, s_patch, down_pos, across, mods, t_out, s_out = refs[:10]
    refs = refs[10:]
    teacher, student, back = refs[:groups], refs[groups : 2 * groups], refs[2 * groups]
    samples, _, tokens = noisy_ref.shape
    for sample in range(samples):
        second_v, _, _, _ = settle(
            teacher, half_ref, t_patch, down_pos, across, mods, t_out, 5, sample
        )
        student_v, final, reciprocal, gate = settle(
            student, noisy_ref, s_patch, down_pos, across, mods, s_out, 8, sample
        )
        noisy, halfway = noisy_ref[sample], half_ref[sample]
        alpha, sigma = coefs[sample, 0], coefs[sample, 1]
        alpha_mid, sigma_mid = coefs[sample, 2], coefs[sample, 3]
        alpha_end, sigma_end = coefs[sample, 4], coefs[sample, 5]
        ratio, gap, push = coefs[sample, 6], coefs[sample, 7], coefs[sample, 8]
        second_x = alpha_mid * halfway - sigma_mid * second_v
        landing = alpha_end * second_x + sigma_end * (halfway - alpha_mid * second_x) / sigma_mid
        target = (landing - ratio * noisy) / gap
        student_x = alpha * noisy - sigma * student_v
        back_velocity = push * (student_x - target)
        high = back_velocity.astype(BF16)
        rest = back_velocity - high.astype(F32)
        mid = rest.astype(BF16)
        low = (rest - mid.astype(F32)).astype(BF16)
        back_final = dot(upright(low), s_out[...], ((1,), (0,)))
        back_final = back_final + dot(upright(mid), s_out[...], ((1,), (0,)))
        back_final = back_final + dot(upright(high), s_out[...], ((1,), (0,)))
        centre = jnp.mean(back_final, axis=-1, keepdims=True)
        along = jnp.mean(back_final * final, axis=-1, keepdims=True)
        back[sample * tokens : (sample + 1) * tokens, :] = (
            gate * (reciprocal * (back_final - centre - final * along))
        ).astype(BF16)


def last(coefs, noisy, halfway, t_patch, s_patch, pos, mods, t_out, s_out, teacher, student):
    groups = len(teacher)
    samples, _, tokens = noisy.shape
    return pl.pallas_call(
        functools.partial(last_kernel, groups),
        out_shape=jax.ShapeDtypeStruct((samples * tokens, t_out.shape[1]), BF16),
        in_specs=[full(pltpu.SMEM)] + [full()] * (9 + 2 * groups),
        out_specs=full(),
        compiler_params=pltpu.CompilerParams(vmem_limit_bytes=VMEM_LIMIT),
        cost_estimate=pl.CostEstimate(flops=2 * 10**9, bytes_accessed=4 * 10**6, transcendentals=0),
        name="last",
    )(coefs, noisy, halfway, t_patch, s_patch, *pos, mods, t_out, s_out, *teacher, *student)


def store_blocks(order, grad, blocks, sem):
    copies = []
    if len(blocks) == 1:
        copies.append(pltpu.make_async_copy(grad, blocks[0], sem.at[0]))
    else:
        mine, other = blocks
        count, rows = mine.shape[0], mine.shape[1]
        for spot in range(2 * count):
            start = pl.multiple_of(order[spot], 8)
            target = (mine, other)[spot % 2].at[spot // 2]
            copies.append(pltpu.make_async_copy(grad.at[pl.ds(start, rows), :], target, sem.at[spot]))
    for copy in copies:
        copy.start()
    for copy in copies:
        copy.wait()


def weight_grad_kernel(groups, outs, *refs):
    order, refs = refs[0], refs[1:]
    backs, hidden, blocks = refs[:groups], refs[groups], refs[groups + 1 : groups + 1 + outs]
    back, grad, sem = refs[groups + 1 + outs :]
    rows = backs[0].shape[0]
    for group in range(groups):
        back[group * rows : (group + 1) * rows, :] = backs[group][...]
    features = back.shape[1]
    tile = column_tile(features)

    def step(index, carry):
        at = pl.multiple_of(index * tile, tile)
        grad[pl.ds(at, tile), :] = dot(back[:, pl.ds(at, tile)], hidden[...], ((0,), (0,)))
        return carry

    lax.fori_loop(0, features // tile, step, 0)
    store_blocks(order, grad, blocks, sem)


def back_pre_kernel(groups, pieces, *refs):
    order, refs = refs[0], refs[1:]
    backs, pre, refs = refs[:groups], refs[groups], refs[groups + 1 :]
    down_pieces, back_pre, back, down, sem = refs[:pieces], *refs[pieces:]
    copies = load_pieces(order, down_pieces, down, sem)
    rows = backs[0].shape[0]
    for group in range(groups):
        back[group * rows : (group + 1) * rows, :] = backs[group][...]
    for copy in copies:
        copy.wait()
    back_hidden = dot(back[...], down[...], ((1,), (0,)))
    back_pre[...] = (back_hidden * gelu_slope(pre[...])).astype(BF16)


def block_shapes(count, features, width):
    if count == 1:
        return [jax.ShapeDtypeStruct((features, width), F32)]
    return [jax.ShapeDtypeStruct((count // 2, features // count, width), F32)] * 2


def weight_grad(order, backs, hidden, count):
    features = backs[0].shape[1]
    total, width = hidden.shape
    shapes = block_shapes(count, features, width)
    return pl.pallas_call(
        functools.partial(weight_grad_kernel, len(backs), len(shapes)),
        out_shape=shapes,
        in_specs=[full(pltpu.SMEM)] + [full()] * (len(backs) + 1),
        out_specs=[full(pltpu.HBM)] * len(shapes),
        scratch_shapes=[
            pltpu.VMEM((total, features), BF16),
            pltpu.VMEM((features, width), F32),
            pltpu.SemaphoreType.DMA((count,)),
        ],
        compiler_params=pltpu.CompilerParams(vmem_limit_bytes=VMEM_LIMIT),
        cost_estimate=pl.CostEstimate(
            flops=2 * total * features * width, bytes_accessed=8 * features * width, transcendentals=0
        ),
    )(order, *backs, hidden)


def back_through(order, backs, pre, down_pieces):
    features = backs[0].shape[1]
    total, width = pre.shape
    pieces = len(down_pieces)
    return pl.pallas_call(
        functools.partial(back_pre_kernel, len(backs), pieces),
        out_shape=jax.ShapeDtypeStruct((total, width), BF16),
        in_specs=[full(pltpu.SMEM)] + [full()] * (len(backs) + 1) + [full(pltpu.HBM)] * pieces,
        out_specs=full(),
        scratch_shapes=[
            pltpu.VMEM((total, features), BF16),
            pltpu.VMEM((features, width), BF16),
            pltpu.SemaphoreType.DMA((pieces,)),
        ],
        compiler_params=pltpu.CompilerParams(vmem_limit_bytes=VMEM_LIMIT),
        cost_estimate=pl.CostEstimate(
            flops=2 * total * features * width, bytes_accessed=8 * features * width, transcendentals=total * width
        ),
        name="back_pre",
    )(order, *backs, pre, *down_pieces)


def after(value, earlier):
    return lax.optimization_barrier((value, earlier))[0]


def swap_plane(value, flip, size):
    return lax.ppermute(value, PLANE, [(spot, spot ^ flip) for spot in range(size)])


def swap_col(value, flip, size):
    return lax.ppermute(value, "col", [(spot, spot ^ flip) for spot in range(size)])


def swap_both(value, flip, plane, columns):
    pairs = []
    for spot in range(plane):
        for col in range(columns):
            pairs.append((spot * columns + col, (spot ^ flip[0]) * columns + (col ^ flip[1])))
    return lax.ppermute(value, ("dp", "row", "col"), pairs)


def chips_of_plane(even, odd, size):
    return [even] + [swap_plane((even, odd)[flip % 2], 2 * flip, size) for flip in range(1, size // 2)]


def both_cores(shards, size):
    pieces = []
    for shard in shards:
        pieces += [shard, swap_plane(shard, 1, size)]
    return pieces


def spread_col(value, size):
    return [value] + [swap_col(value, flip, size) for flip in range(1, size)]


def condition(times, embedded, offset, rows):
    half = D // 2
    places = offset + jnp.arange(rows, dtype=jnp.int32)
    low = places < half
    power = jnp.where(low, places, places - half).astype(F32)
    freqs = jnp.exp(-math.log(10000.0) * power / half)
    angle = (1000.0 * times)[:, None] * freqs[None, :]
    features = jnp.where(low[None, :], jnp.cos(angle), jnp.sin(angle))
    return jax.nn.silu(embedded + features).astype(BF16)


def modulation_part(labels, step_index, class_table, teacher_mod, student_mod, earlier, fast, plane):
    rows = teacher_mod.shape[0]
    packed = labels * 16 + step_index
    if fast:
        others = [swap_plane(packed, flip, plane) for flip in range(1, plane)]
        everyone = jnp.concatenate([packed] + others, axis=0)
    else:
        everyone = lax.all_gather(packed, PLANE, axis=0, tiled=True)
    everyone = after(everyone, earlier)
    all_labels, all_steps = everyone // 16, everyone % 16
    all_now = all_steps.astype(F32) / STEPS
    offset = lax.axis_index(PLANE) * rows
    table = lax.dynamic_slice_in_dim(class_table, offset, rows, 1)
    onehot = (all_labels[:, None] == jnp.arange(CLASSES, dtype=jnp.int32)[None, :]).astype(BF16)
    embedded = jnp.dot(onehot, table, preferred_element_type=F32)
    rows_now = condition(all_now, embedded, offset, rows)
    rows_mid = condition(all_now - 0.5 / STEPS, embedded, offset, rows)
    count = rows_now.shape[0]
    share = teacher_mod.shape[2]
    teacher_flat = teacher_mod.reshape(rows, 3 * share)
    student_flat = student_mod.reshape(rows, 3 * share)
    teacher_part = jnp.dot(
        jnp.concatenate([rows_now, rows_mid], axis=0), teacher_flat, preferred_element_type=F32
    )
    student_part = jnp.dot(rows_now, student_flat, preferred_element_type=F32)
    return jnp.concatenate([teacher_part[:count], teacher_part[count:], student_part], axis=1)


def modulation_sum(part, samples, fast, square, plane):
    if not fast:
        return lax.psum_scatter(part, PLANE, scatter_dimension=0, tiled=True)[None]
    part = part.reshape(plane // 2, 2, samples, part.shape[1])
    pair = part[:, 0] + swap_plane(part[:, 1], 1, plane)
    sets = 2 if square else 1
    own = jnp.stack([pair[other] for other in range(sets)], axis=0)
    for flip in range(1, plane // 2):
        sent = jnp.stack([pair[flip ^ other] for other in range(sets)], axis=0)
        own = own + swap_plane(sent, 2 * flip, plane)
    return own


def modulation_columns(own, columns, col):
    sets, samples = own.shape[:2]
    own = own.reshape(sets * samples, 9, own.shape[2] // 9)
    gathered = spread_col(own, columns)
    ordered = []
    for place_at in range(columns):
        piece = gathered[place_at]
        for other in range(1, columns):
            piece = jnp.where(col == other, gathered[place_at ^ other], piece)
        ordered.append(piece)
    return jnp.concatenate(ordered, axis=2)


def positions(chunks, tokens):
    quarter = D // 4
    omega = 1.0 / 10000.0 ** (jnp.arange(quarter, dtype=F32) / quarter)
    side = math.isqrt(SEQ)
    span = tokens // side
    angle = jnp.arange(side, dtype=F32)[:, None] * omega[None, :]
    across = jnp.concatenate([jnp.zeros((side, D // 2), F32), jnp.sin(angle), jnp.cos(angle)], axis=1)
    grid_rows = chunks[:, None] * span + jnp.arange(span, dtype=jnp.int32)
    turn = grid_rows.astype(F32)[:, :, None] * omega
    down = jnp.concatenate(
        [jnp.sin(turn), jnp.cos(turn), jnp.zeros((chunks.shape[0], span, D // 2), F32)], axis=2
    )
    return down, across


def body(
    latents,
    labels,
    step_index,
    seeds,
    class_table,
    teacher_patch,
    teacher_mod,
    teacher_up,
    teacher_down,
    teacher_out,
    student_patch,
    student_mod,
    student_up,
    student_down,
    student_out,
):
    samples = latents.shape[0]
    plane = lax.axis_size(PLANE)
    columns = lax.axis_size("col")
    batch_total = samples * plane
    col = lax.axis_index("col")
    spot = lax.axis_index(PLANE)
    rows = teacher_up.shape[0]
    tokens = SEQ // columns
    fast = rows % 16 == 0 and plane <= 8
    count = plane if fast else 1

    order = ((jnp.arange(count, dtype=jnp.int32) ^ spot) * rows).astype(jnp.int32)

    square = fast and columns == 4 and plane >= 4
    odd_chip = (spot // 2) % 2 == 1

    def chips(even, odd=None):
        if fast:
            return chips_of_plane(even, even if odd is None else odd, plane)
        return [lax.all_gather(even, PLANE, axis=0, tiled=True)]

    def cores(shards):
        return both_cores(shards, plane) if fast else shards

    def teacher_shards(shard, abroad):
        if not square:
            return (shard,)
        return jnp.where(odd_chip, abroad, shard), jnp.where(odd_chip, shard, abroad)

    up_abroad = swap_col(teacher_up, 2, columns) if square else teacher_up
    down_abroad = swap_col(after(teacher_down, up_abroad), 2, columns) if square else teacher_down
    student_up_shards = chips(student_up)
    up_sent = teacher_shards(teacher_up, up_abroad)
    up_shards = chips(*up_sent)
    part = modulation_part(
        labels, step_index, class_table, teacher_mod, student_mod, up_sent, fast, plane
    )
    own_mods = modulation_sum(part, samples, fast, square, plane)
    mods = modulation_columns(own_mods, columns, col)
    teacher_up_pieces = cores(up_shards)
    down_shards = chips(*after(teacher_shards(teacher_down, down_abroad), up_shards))
    teacher_down_pieces = cores(after(down_shards, mods))
    student_down_shards = chips(after(student_down, own_mods))
    latents, seeds, col, step_index = after((latents, seeds, col, step_index), part)

    if square:
        members = [(0, 0), (0, 1), (2, 0), (2, 1)]
    else:
        members = [(0, flip) for flip in range(columns)]
    chunks = jnp.arange(columns, dtype=jnp.int32) ^ col
    pos = positions(chunks, tokens)
    now = step_index.astype(F32) / STEPS
    alpha, sigma = plan(now)
    alpha_mid, sigma_mid = plan(now - 0.5 / STEPS)
    alpha_end, sigma_end = plan(now - 1.0 / STEPS)
    ratio = sigma_end / sigma
    weight = jnp.maximum(alpha * alpha / (sigma * sigma), 1.0)
    push = -2.0 * sigma * weight / batch_total
    values = [alpha, sigma, alpha_mid, sigma_mid, alpha_end, sigma_end, ratio, alpha_end - ratio * alpha, push]
    lane = lax.broadcasted_iota(jnp.int32, (samples, len(values)), 1)
    coefs = jnp.zeros((samples, len(values)), F32)
    for place_at, value in enumerate(values):
        coefs = jnp.where(lane == place_at, value[:, None], coefs)
    clean = latents.reshape(samples, columns, tokens, PATCH)
    clean = jnp.take(jnp.transpose(clean, (1, 0, 3, 2)), chunks, axis=0)
    token = chunks[:, None, None, None] * tokens + jnp.arange(tokens, dtype=jnp.int32)
    places = token * PATCH + jnp.arange(PATCH, dtype=jnp.int32)[None, None, :, None]
    shaped = (1, samples, 1, 1)
    noisy = alpha.reshape(shaped) * clean + sigma.reshape(shaped) * noise_at(
        seeds.reshape(shaped), places
    )

    def share(parts, flips):
        return [parts[0]] + [
            swap_both(part, flip, plane, columns) for part, flip in zip(parts[1:], flips[1:])
        ]

    def teach(state, first_mod):
        return forward(
            order, state, teacher_patch, teacher_pos, mods, teacher_up_pieces, teacher_down_pieces,
            first_mod, False, 2 if square else 0,
        )

    teacher_pos, teacher_noisy = pos, noisy
    if square:
        near = noisy[:2]
        teacher_noisy = jnp.concatenate([near, swap_plane(near, 2, plane)], axis=0)
        teacher_pos = (jnp.concatenate([pos[0][:2], pos[0][:2]], axis=0), pos[1])
    line = [(0, flip) for flip in range(columns)]
    parts = teach(teacher_noisy, 0)
    first = share(parts, members)
    student_up_pieces = cores(after(student_up_shards, parts))
    student_down_pieces = cores(after(student_down_shards, parts))
    saved = forward(order, noisy, student_patch, pos, mods, student_up_pieces, student_down_pieces, 6, True)
    halfway = middle(coefs, noisy[0], teacher_patch, pos, mods, teacher_out, after(first, saved))
    half_all = jnp.stack([halfway] + [swap_both(halfway, flip, plane, columns) for flip in members[1:]], axis=0)
    student_parts = after(saved[:columns], half_all)
    second = share(teach(half_all, 3), members)
    student = share(student_parts, line)
    act, pre, hidden = saved[columns:]
    back = last(
        coefs,
        noisy[0],
        halfway,
        teacher_patch,
        student_patch,
        pos,
        mods,
        teacher_out,
        student_out,
        second,
        student,
    )
    backs = spread_col(back, columns)

    def pair_sum(blocks):
        if not fast:
            return blocks[0]
        mine, other = blocks
        return mine + swap_plane(other, 1, plane)

    def chip_sum(pair):
        if not fast:
            return lax.psum_scatter(pair, PLANE, scatter_dimension=0, tiled=True)
        total = pair[0]
        for flip in range(1, plane // 2):
            total = total + swap_plane(pair[flip].astype(BF16), 2 * flip, plane).astype(F32)
        return total

    down_blocks = weight_grad(order, backs, hidden, count)
    back_pre = back_through(order, backs, after(pre, down_blocks), student_down_pieces)
    down_pair = pair_sum(down_blocks)
    up_blocks = weight_grad(order, [after(act, down_pair)], back_pre, count)
    up_gradient = chip_sum(pair_sum(up_blocks))
    down_gradient = chip_sum(down_pair)
    return (up_gradient, down_gradient)


def solution(mesh):
    rows = P(("dp", "row"), "col")
    mod = P(("dp", "row"), None, "col")
    batch = P(("dp", "row"))
    placed = (
        P(("dp", "row"), None, None),
        batch,
        batch,
        batch,
        P(),
        P(),
        mod,
        rows,
        rows,
        P(),
        P(),
        mod,
        rows,
        rows,
        P(),
    )

    return jax.shard_map(body, mesh=mesh, in_specs=placed, out_specs=(rows, rows), check_vma=False)
```

profile of v0, /device:TPU:0, one launch (start us, length us, event | category | flops | bytes accessed | tf_op | source)
XLA Modules:
  0.0 281.4 jit_solution(18219687666421001360)
XLA Ops:
  2.0 2.5 collective-permute-start.1
  6.3 2.6 collective-permute-start.7
  13.3 2.3 collective-permute-start.5
  19.6 4.8 %collective-permute-done.7 = bf16[144,1152]{1,0:T(8,128)(2,1)} collective-permute-done((bf16[144,1152]{1,0:T(8,128)(2,1)}, bf16[144,1152]{1,0:T(8,128)(2,1)}, u32[]{:S(2)}, u32[]{:S(2)}) %collective-permute-start.7) | collective-permute-done | bytes 331808 | tf_op jit(solution)/shard_map/ppermute | solution.py:391
  35.7 12.3 %collective-permute-done.26 = bf16[144,1152]{1,0:T(8,128)(2,1)S(1)} collective-permute-done((bf16[144,1152]{1,0:T(8,128)(2,1)}, bf16[144,1152]{1,0:T(8,128)(2,1)S(1)}, u32[]{:S(2)}, u32[]{:S(2)}) %collective-permute-start.26) | collective-permute-done | bytes 331808 | tf_op jit(solution)/shard_map/ppermute | solution.py:391
  56.7 2.3 collective-permute-start.14
  60.2 2.7 collective-permute-done.12
  62.9 4.9 %collective-permute-done.13 = f32[6,9,288]{2,1,0:T(8,128)S(1)} collective-permute-done((f32[6,9,288]{2,1,0:T(8,128)S(1)}, f32[6,9,288]{2,1,0:T(8,128)S(1)}, u32[]{:S(2)}, u32[]{:S(2)}) %collective-permute-start.13) | collective-permute-done | bytes 62240 | tf_op jit(solution)/shard_map/ppermute | solution.py:391
  74.4 3.0 %collective-permute-done.29.refs_20_ = bf16[144,1152]{1,0:T(8,128)(2,1)} collective-permute-done((bf16[144,1152]{1,0:T(8,128)(2,1)}, bf16[144,1152]{1,0:T(8,128)(2,1)}, u32[]{:S(2)}, u32[]{:S(2)}) %collective-permute-start.29) | collective-permute-done | bytes 331808 | tf_op jit(solution)/shard_map/ppermute | solution.py:387
  88.1 11.4 %shard_map.158 = (bf16[192,1152]{1,0:T(8,128)(2,1)S(1)}, bf16[192,1152]{1,0:T(8,128)(2,1)S(1)}, bf16[192,1152]{1,0:T(8,128)(2,1)S(1)}, bf16[192,1152]{1,0:T(8,128)(2,1)S(1)}) custom-call(s32[8]{0:T(128)S(1)} %xor_multiply_fusion.refs_0_, f32[4,3,16,64]{3,2,1,0:T(8,128)S(1)} %pad_maximum_fusion.refs_1_, bf16[16,1152]{1,0:T(8,128)(2,1)S(1)} %copy-done.14, ...), custom_call_target="tpu_custom_call" | custom-call | flops 4076863488 | bytes 10616832 | tf_op jit(solution)/shard_map/pallas_call | solution.py:181
  99.6 2.2 collective-permute-start.17
  101.7 4.9 %collective-permute-done.40.refs_20_.refs_12_ = bf16[144,1152]{1,0:T(8,128)(2,1)S(1)} collective-permute-done((bf16[144,1152]{1,0:T(8,128)(2,1)S(1)}, bf16[144,1152]{1,0:T(8,128)(2,1)S(1)}, u32[]{:S(2)}, u32[]{:S(2)}) %collective-permute-start.40) | collective-permute-done | bytes 331808 | tf_op jit(solution)/shard_map/ppermute | solution.py:387
  107.7 4.8 %collective-permute-done.17.refs_12_ = bf16[144,1152]{1,0:T(8,128)(2,1)S(1)} collective-permute-done((bf16[144,1152]{1,0:T(8,128)(2,1)S(1)}, bf16[144,1152]{1,0:T(8,128)(2,1)S(1)}, u32[]{:S(2)}, u32[]{:S(2)}) %collective-permute-start.17) | collective-permute-done | bytes 331808 | tf_op jit(solution)/shard_map/ppermute | solution.py:387
  117.3 11.9 %shard_map.159 = (bf16[192,1152]{1,0:T(8,128)(2,1)S(1)}, bf16[192,1152]{1,0:T(8,128)(2,1)S(1)}, bf16[192,1152]{1,0:T(8,128)(2,1)S(1)}, bf16[192,1152]{1,0:T(8,12...) custom-call(s32[8]{0:T(128)S(1)} %xor_multiply_fusion.refs_0_, ...), custom_call_target="tpu_custom_call" | custom-call | flops 4076863488 | bytes 10616832 | tf_op jit(solution)/shard_map/pallas_call | solution.py:181
  129.2 6.7 %collective-permute-done.46.refs_9_ = bf16[192,1152]{1,0:T(8,128)(2,1)S(1)} collective-permute-done((bf16[192,1152]{1,0:T(8,128)(2,1)S(1)}, bf16[192,1152]{1,0:T(8,128)(2,1)S(1)}, u32[]{:S(2)}, u32[]{:S(2)}) %collective-permute-start.46) | collective-permute-done | bytes 442400 | tf_op jit(solution)/shard_map/ppermute | solution.py:399
  148.9 11.4 %shard_map.160 = (bf16[192,1152]{1,0:T(8,128)(2,1)S(1)}, bf16[192,1152]{1,0:T(8,128)(2,1)S(1)}, bf16[192,1152]{1,0:T(8,128)(2,1)S(1)}, bf16[192,1152]{1,0:T(8,128)(2,1)S(1)}) custom-call(s32[8]{0:T(128)S(1)} %xor_multiply_fusion.refs_0_, f32[4,3,16,64]{3,2,1,0:T(8,128)S(1)} %pad_maximum_fusion.1.refs_1_, bf16[16,1152]{1,0:T(8,128)(2,1)S(1)} %copy-done.14, ...), custom_call_target="tpu_custom_call" | custom-call | flops 4076863488 | bytes 10616832 | tf_op jit(solution)/shard_map/pallas_call | solution.py:181
  162.0 3.3 %collective-permute-done.54.refs_15_ = bf16[192,1152]{1,0:T(8,128)(2,1)S(1)} collective-permute-done((bf16[192,1152]{1,0:T(8,128)(2,1)S(1)}, bf16[192,1152]{1,0:T(8,128)(2,1)S(1)}, u32[]{:S(2)}, u32[]{:S(2)}) %collective-permute-start.54) | collective-permute-done | bytes 442400 | tf_op jit(solution)/shard_map/ppermute | solution.py:399
  165.3 13.3 %collective-permute-done.55.refs_16_ = bf16[192,1152]{1,0:T(8,128)(2,1)S(1)} collective-permute-done((bf16[192,1152]{1,0:T(8,128)(2,1)S(1)}, bf16[192,1152]{1,0:T(8,128)(2,1)S(1)}, u32[]{:S(2)}, u32[]{:S(2)}) %collective-permute-start.55) | collective-permute-done | bytes 442400 | tf_op jit(solution)/shard_map/ppermute | solution.py:399
  178.6 6.1 %collective-permute-done.51.refs_11_ = bf16[192,1152]{1,0:T(8,128)(2,1)S(1)} collective-permute-done((bf16[192,1152]{1,0:T(8,128)(2,1)S(1)}, bf16[192,1152]{1,0:T(8,128)(2,1)S(1)}, u32[]{:S(2)}, u32[]{:S(2)}) %collective-permute-start.51) | collective-permute-done | bytes 442400 | tf_op jit(solution)/shard_map/ppermute | solution.py:399
  184.8 7.3 %collective-permute-done.53.refs_13_ = bf16[192,1152]{1,0:T(8,128)(2,1)S(1)} collective-permute-done((bf16[192,1152]{1,0:T(8,128)(2,1)S(1)}, bf16[192,1152]{1,0:T(8,128)(2,1)S(1)}, u32[]{:S(2)}, u32[]{:S(2)}) %collective-permute-start.53) | collective-permute-done | bytes 442400 | tf_op jit(solution)/shard_map/ppermute | solution.py:399
  192.1 5.3 %last.1.refs_1_ = bf16[192,1152]{1,0:T(8,128)(2,1)S(1)} custom-call(f32[3,9]{1,0:T(4,128)S(1)} %select_select_fusion.4.refs_0_, f32[3,16,64]{2,1,0:T(8,128)S(1)} %slice_bitcast_fusion.10.refs_1_, f32[3,16,64]{2,1,0:T(8,128)S(1)} %middle.1.refs_2_, bf16[16,1152]{1,0:T(8,128)(2,1)S(1)} %copy-done.14, bf16[16,1152]{1,0:T(8,128)(2,1)S(1)} %copy-done.13, ...), custom_call_target="tpu_custom_call" | custom-call | flops 2000000000 | bytes 4000000 | tf_op jit(solution)/shard_map/last/pallas_call | solution.py:272
  198.7 2.8 %collective-permute-start.58 = (bf16[192,1152]{1,0:T(8,128)(2,1)S(1)}, bf16[192,1152]{1,0:T(8,128)(2,1)S(1)}, u32[]{:S(2)}, u32[]{:S(2)}) collective-permute-start(bf16[192,1152]{1,0:T(8,128)(2,1)S(1)} %last.1.refs_1_), channel_id=1, source_target_pairs={{0,2},{1,3},{2,0},{3,1},{4,6},{5,7},{6,4},{7,5},{8,10},{9,11},{10,... | collective-permute-start | bytes 1327112 | tf_op jit(solution)/shard_map/ppermute | solution.py:391
  201.8 14.5 %collective-permute-done.57.refs_2_ = bf16[192,1152]{1,0:T(8,128)(2,1)S(1)} collective-permute-done((bf16[192,1152]{1,0:T(8,128)(2,1)S(1)}, bf16[192,1152]{1,0:T(8,128)(2,1)S(1)}, u32[]{:S(2)}, u32[]{:S(2)}) %collective-permute-start.57) | collective-permute-done | bytes 442400 | tf_op jit(solution)/shard_map/ppermute | solution.py:391
  216.3 15.2 %collective-permute-done.58.refs_3_ = bf16[192,1152]{1,0:T(8,128)(2,1)S(1)} collective-permute-done((bf16[192,1152]{1,0:T(8,128)(2,1)S(1)}, bf16[192,1152]{1,0:T(8,128)(2,1)S(1)}, u32[]{:S(2)}, u32[]{:S(2)}) %collective-permute-start.58) | collective-permute-done | bytes 442400 | tf_op jit(solution)/shard_map/ppermute | solution.py:391
  231.6 4.9 %shard_map.161 = (f32[4,144,1152]{2,1,0:T(8,128)S(1)}, f32[4,144,1152]{2,1,0:T(8,128)S(1)}) custom-call(s32[8]{0:T(128)S(1)} %xor_multiply_fusion.refs_0_, bf16[192,1152]{1,0:T(8,128)(2,1)S(1)} %last.1.refs_1_, bf16[192,1152]{1,0:T(8,128)(2,1)S(1)} %collective-permute-done.57.refs_2_, bf16[192,1152]{1,0:T(8,128)(2,1)S(1)} %collective-permute-done.58.refs_3_, ...), custom_call_target="tpu_custom_call" | custom-call | flops 2038431744 | bytes 10616832 | tf_op jit(solution)/shard_map/pallas_call | solution.py:343
  236.6 5.5 %back_pre.1.refs_2_ = bf16[768,1152]{1,0:T(8,128)(2,1)S(1)} custom-call(s32[8]{0:T(128)S(1)} %xor_multiply_fusion.refs_0_, bf16[192,1152]{1,0:T(8,128)(2,1)S(1)} %last.1.refs_1_, bf16[192,1152]{1,0:T(8,128)(2,1)S(1)} %collective-permute-done.57.refs_2_, bf16[192,1152]{1,0:T(8,128)(2,1)S(1)} %collective-permute-done.58.refs_3_, ...), custom_call_target="tpu_custom_call" | custom-call | flops 2038431744 | bytes 10616832 | tf_op jit(solution)/shard_map/back_pre/pallas_call | solution.py:364
  242.5 4.9 %shard_map.162 = (f32[4,144,1152]{2,1,0:T(8,128)S(1)}, f32[4,144,1152]{2,1,0:T(8,128)S(1)}) custom-call(s32[8]{0:T(128)S(1)} %xor_multiply_fusion.refs_0_, bf16[768,1152]{1,0:T(8,128)(2,1)S(1)} %get-tuple-element.98.refs_1_, bf16[768,1152]{1,0:T(8,128)(2,1)S(1)} %back_pre.1.refs_2_), custom_call_target="tpu_custom_call" | custom-call | flops 2038431744 | bytes 10616832 | tf_op jit(solution)/shard_map/pallas_call | solution.py:343
  255.5 4.3 %collective-permute-done.65 = bf16[144,1152]{1,0:T(8,128)(2,1)S(1)} collective-permute-done((bf16[144,1152]{1,0:T(8,128)(2,1)S(1)}, bf16[144,1152]{1,0:T(8,128)(2,1)S(1)}, u32[]{:S(2)}, u32[]{:S(2)}) %collective-permute-start.65) | collective-permute-done | bytes 331808 | tf_op jit(solution)/shard_map/ppermute | solution.py:387
  261.6 5.8 %collective-permute-done.67 = bf16[144,1152]{1,0:T(8,128)(2,1)S(1)} collective-permute-done((bf16[144,1152]{1,0:T(8,128)(2,1)S(1)}, bf16[144,1152]{1,0:T(8,128)(2,1)S(1)}, u32[]{:S(2)}, u32[]{:S(2)}) %collective-permute-start.67) | collective-permute-done | bytes 331808 | tf_op jit(solution)/shard_map/ppermute | solution.py:387
  268.4 3.7 %collective-permute-done.62 = bf16[144,1152]{1,0:T(8,128)(2,1)S(1)} collective-permute-done((bf16[144,1152]{1,0:T(8,128)(2,1)S(1)}, bf16[144,1152]{1,0:T(8,128)(2,1)S(1)}, u32[]{:S(2)}, u32[]{:S(2)}) %collective-permute-start.62) | collective-permute-done | bytes 331808 | tf_op jit(solution)/shard_map/ppermute | solution.py:387
  272.1 2.5 collective-permute-done.63
  274.6 5.9 %collective-permute-done.64 = bf16[144,1152]{1,0:T(8,128)(2,1)S(1)} collective-permute-done((bf16[144,1152]{1,0:T(8,128)(2,1)S(1)}, bf16[144,1152]{1,0:T(8,128)(2,1)S(1)}, u32[]{:S(2)}, u32[]{:S(2)}) %collective-permute-start.64) | collective-permute-done | bytes 331808 | tf_op jit(solution)/shard_map/ppermute | solution.py:387
  (248 shorter events, 84.1 us)
Async XLA Ops:
  6.3 18.0 %collective-permute-start.7 = (bf16[144,1152]{1,0:T(8,128)(2,1)}, bf16[144,1152]{1,0:T(8,128)(2,1)}, u32[]{:S(2)}, u32[]{:S(2)}) collective-permute-start(bf16[144,1152]{1,0:T(8,128)(2,1)} %param.22), channel_id=1, source_target_pairs={{0,2},{1,3},{2,0},{3,1},{4,6},{5,7},{6,4},{7,5},{8,10},{9,11},{10,... | collective-permute-start | bytes 995336 | tf_op jit(solution)/shard_map/ppermute | solution.py:391
  26.1 23.4 %collective-permute-start.20 = (bf16[144,1152]{1,0:T(8,128)(2,1)}, bf16[144,1152]{1,0:T(8,128)(2,1)S(1)}, u32[]{:S(2)}, u32[]{:S(2)}) collective-permute-start(bf16[144,1152]{1,0:T(8,128)(2,1)} %get-tuple-element.118), channel_id=1, source_target_pairs={{0,8},{4,12},{8,0},{12,4},{16,24},{20,28},{24,16},{28,20},{1,9},{5... | collective-permute-start | bytes 995336 | tf_op jit(solution)/shard_map/ppermute | solution.py:387
  27.7 25.2 %collective-permute-start.24 = (bf16[144,1152]{1,0:T(8,128)(2,1)}, bf16[144,1152]{1,0:T(8,128)(2,1)}, u32[]{:S(2)}, u32[]{:S(2)}) collective-permute-start(bf16[144,1152]{1,0:T(8,128)(2,1)} %get-tuple-element.118), channel_id=1, source_target_pairs={{0,24},{4,28},{8,16},{12,20},{16,8},{20,12},{24,0},{28,4},{1,25},{... | collective-permute-start | bytes 995336 | tf_op jit(solution)/shard_map/ppermute | solution.py:387
  28.1 24.7 %collective-permute-start.22 = (bf16[144,1152]{1,0:T(8,128)(2,1)S(1)}, bf16[144,1152]{1,0:T(8,128)(2,1)}, u32[]{:S(2)}, u32[]{:S(2)}) collective-permute-start(bf16[144,1152]{1,0:T(8,128)(2,1)S(1)} %get-tuple-element.119.refs_6_), channel_id=1, source_target_pairs={{0,16},{4,20},{8,24},{12,28},{16,0},{20,4},{24,8},{28,12},{1,17},{... | collective-permute-start | bytes 995336 | tf_op jit(solution)/shard_map/ppermute | solution.py:387
  31.7 16.3 %collective-permute-start.26 = (bf16[144,1152]{1,0:T(8,128)(2,1)}, bf16[144,1152]{1,0:T(8,128)(2,1)S(1)}, u32[]{:S(2)}, u32[]{:S(2)}) collective-permute-start(bf16[144,1152]{1,0:T(8,128)(2,1)} %param.23), channel_id=1, source_target_pairs={{0,2},{1,3},{2,0},{3,1},{4,6},{5,7},{6,4},{7,5},{8,10},{9,11},{10,... | collective-permute-start | bytes 995336 | tf_op jit(solution)/shard_map/ppermute | solution.py:391
  34.1 19.2 %collective-permute-start.9 = (f32[2,3,2592]{2,1,0:T(4,128)S(1)}, f32[2,3,2592]{2,1,0:T(4,128)S(1)}, u32[]{:S(2)}, u32[]{:S(2)}) collective-permute-start(f32[2,3,2592]{2,1,0:T(4,128)S(1)} %pad_maximum_fusion.2), channel_id=1, source_target_pairs={{0,8},{4,12},{8,0},{12,4},{16,24},{20,28},{24,16},{28,20},{1,9},{5... | collective-permute-start | bytes 186632 | tf_op jit(solution)/shard_map/ppermute | solution.py:387
  52.8 15.8 %collective-permute-start.27 = (bf16[144,1152]{1,0:T(8,128)(2,1)}, bf16[144,1152]{1,0:T(8,128)(2,1)S(1)}, u32[]{:S(2)}, u32[]{:S(2)}) collective-permute-start(bf16[144,1152]{1,0:T(8,128)(2,1)} %get-tuple-element.59), channel_id=1, source_target_pairs={{0,8},{4,12},{8,0},{12,4},{16,24},{20,28},{24,16},{28,20},{1,9},{5... | collective-permute-start | bytes 995336 | tf_op jit(solution)/shard_map/ppermute | solution.py:387
  56.7 11.9 %collective-permute-start.14 = (f32[6,9,288]{2,1,0:T(8,128)S(1)}, f32[6,9,288]{2,1,0:T(8,128)S(1)}, u32[]{:S(2)}, u32[]{:S(2)}) collective-permute-start(f32[6,9,288]{2,1,0:T(8,128)S(1)} %reshape.157), channel_id=1, source_target_pairs={{0,1},{1,0},{2,3},{3,2},{4,5},{5,4},{6,7},{7,6},{8,9},{9,8},{10,11... | collective-permute-start | bytes 186632 | tf_op jit(solution)/shard_map/ppermute | solution.py:391
  62.9 15.4 %collective-permute-start.19 = (bf16[144,1152]{1,0:T(8,128)(2,1)S(1)}, bf16[144,1152]{1,0:T(8,128)(2,1)S(1)}, u32[]{:S(2)}, u32[]{:S(2)}) collective-permute-start(bf16[144,1152]{1,0:T(8,128)(2,1)S(1)} %get-tuple-element.119.refs_6_), channel_id=1, source_target_pairs={{0,4},{4,0},{8,12},{12,8},{16,20},{20,16},{24,28},{28,24},{1,5},{5... | collective-permute-start | bytes 995336 | tf_op jit(solution)/shard_map/ppermute | solution.py:387
  80.2 26.9 %collective-permute-start.15 = (bf16[144,1152]{1,0:T(8,128)(2,1)S(1)}, bf16[144,1152]{1,0:T(8,128)(2,1)S(1)}, u32[]{:S(2)}, u32[]{:S(2)}) collective-permute-start(bf16[144,1152]{1,0:T(8,128)(2,1)S(1)} %copy-done.3), channel_id=1, source_target_pairs={{0,8},{4,12},{8,0},{12,4},{16,24},{20,28},{24,16},{28,20},{1,9},{5... | collective-permute-start | bytes 995336 | tf_op jit(solution)/shard_map/ppermute | solution.py:387
  80.8 26.4 %collective-permute-start.16 = (bf16[144,1152]{1,0:T(8,128)(2,1)S(1)}, bf16[144,1152]{1,0:T(8,128)(2,1)S(1)}, u32[]{:S(2)}, u32[]{:S(2)}) collective-permute-start(bf16[144,1152]{1,0:T(8,128)(2,1)S(1)} %copy-done.3), channel_id=1, source_target_pairs={{0,16},{4,20},{8,24},{12,28},{16,0},{20,4},{24,8},{28,12},{1,17},{... | collective-permute-start | bytes 995336 | tf_op jit(solution)/shard_map/ppermute | solution.py:387
  81.6 17.9 %collective-permute-start.38 = (bf16[144,1152]{1,0:T(8,128)(2,1)S(1)}, bf16[144,1152]{1,0:T(8,128)(2,1)S(1)}, u32[]{:S(2)}, u32[]{:S(2)}) collective-permute-start(bf16[144,1152]{1,0:T(8,128)(2,1)S(1)} %copy-done.2), channel_id=1, source_target_pairs={{0,8},{4,12},{8,0},{12,4},{16,24},{20,28},{24,16},{28,20},{1,9},{5... | collective-permute-start | bytes 995336 | tf_op jit(solution)/shard_map/ppermute | solution.py:387
  83.2 18.5 %collective-permute-start.39 = (bf16[144,1152]{1,0:T(8,128)(2,1)S(1)}, bf16[144,1152]{1,0:T(8,128)(2,1)S(1)}, u32[]{:S(2)}, u32[]{:S(2)}) collective-permute-start(bf16[144,1152]{1,0:T(8,128)(2,1)S(1)} %copy-done.2), channel_id=1, source_target_pairs={{0,16},{4,20},{8,24},{12,28},{16,0},{20,4},{24,8},{28,12},{1,17},{... | collective-permute-start | bytes 995336 | tf_op jit(solution)/shard_map/ppermute | solution.py:387
  84.3 22.3 %collective-permute-start.40 = (bf16[144,1152]{1,0:T(8,128)(2,1)S(1)}, bf16[144,1152]{1,0:T(8,128)(2,1)S(1)}, u32[]{:S(2)}, u32[]{:S(2)}) collective-permute-start(bf16[144,1152]{1,0:T(8,128)(2,1)S(1)} %copy-done.2), channel_id=1, source_target_pairs={{0,24},{4,28},{8,16},{12,20},{16,8},{20,12},{24,0},{28,4},{1,25},{... | collective-permute-start | bytes 995336 | tf_op jit(solution)/shard_map/ppermute | solution.py:387
  99.6 13.0 %collective-permute-start.17 = (bf16[144,1152]{1,0:T(8,128)(2,1)S(1)}, bf16[144,1152]{1,0:T(8,128)(2,1)S(1)}, u32[]{:S(2)}, u32[]{:S(2)}) collective-permute-start(bf16[144,1152]{1,0:T(8,128)(2,1)S(1)} %copy-done.3), channel_id=1, source_target_pairs={{0,24},{4,28},{8,16},{12,20},{16,8},{20,12},{24,0},{28,4},{1,25},{... | collective-permute-start | bytes 995336 | tf_op jit(solution)/shard_map/ppermute | solution.py:387
  113.6 15.6 %collective-permute-start.45 = (bf16[192,1152]{1,0:T(8,128)(2,1)S(1)}, bf16[192,1152]{1,0:T(8,128)(2,1)S(1)}, u32[]{:S(2)}, u32[]{:S(2)}) collective-permute-start(bf16[192,1152]{1,0:T(8,128)(2,1)S(1)} %get-tuple-element.65), channel_id=1, source_target_pairs={{0,1},{1,0},{2,3},{3,2},{4,5},{5,4},{6,7},{7,6},{8,9},{9,8},{10,11... | collective-permute-start | bytes 1327112 | tf_op jit(solution)/shard_map/ppermute | solution.py:399
  114.4 21.4 %collective-permute-start.46 = (bf16[192,1152]{1,0:T(8,128)(2,1)S(1)}, bf16[192,1152]{1,0:T(8,128)(2,1)S(1)}, u32[]{:S(2)}, u32[]{:S(2)}) collective-permute-start(bf16[192,1152]{1,0:T(8,128)(2,1)S(1)} %get-tuple-element.66), channel_id=1, source_target_pairs={{0,8},{1,9},{2,10},{3,11},{4,12},{5,13},{6,14},{7,15},{8,0},{9,1},... | collective-permute-start | bytes 1327112 | tf_op jit(solution)/shard_map/ppermute | solution.py:399
  115.0 20.9 %collective-permute-start.47 = (bf16[192,1152]{1,0:T(8,128)(2,1)S(1)}, bf16[192,1152]{1,0:T(8,128)(2,1)S(1)}, u32[]{:S(2)}, u32[]{:S(2)}) collective-permute-start(bf16[192,1152]{1,0:T(8,128)(2,1)S(1)} %get-tuple-element.67), channel_id=1, source_target_pairs={{0,9},{1,8},{2,11},{3,10},{4,13},{5,12},{6,15},{7,14},{8,1},{9,0},... | collective-permute-start | bytes 1327112 | tf_op jit(solution)/shard_map/ppermute | solution.py:399
  144.5 20.8 %collective-permute-start.54 = (bf16[192,1152]{1,0:T(8,128)(2,1)S(1)}, bf16[192,1152]{1,0:T(8,128)(2,1)S(1)}, u32[]{:S(2)}, u32[]{:S(2)}) collective-permute-start(bf16[192,1152]{1,0:T(8,128)(2,1)S(1)} %get-tuple-element.93), channel_id=1, source_target_pairs={{0,1},{1,0},{2,3},{3,2},{4,5},{5,4},{6,7},{7,6},{8,9},{9,8},{10,11... | collective-permute-start | bytes 1327112 | tf_op jit(solution)/shard_map/ppermute | solution.py:399
  145.7 32.9 %collective-permute-start.55 = (bf16[192,1152]{1,0:T(8,128)(2,1)S(1)}, bf16[192,1152]{1,0:T(8,128)(2,1)S(1)}, u32[]{:S(2)}, u32[]{:S(2)}) collective-permute-start(bf16[192,1152]{1,0:T(8,128)(2,1)S(1)} %get-tuple-element.94), channel_id=1, source_target_pairs={{0,2},{1,3},{2,0},{3,1},{4,6},{5,7},{6,4},{7,5},{8,10},{9,11},{10,... | collective-permute-start | bytes 1327112 | tf_op jit(solution)/shard_map/ppermute | solution.py:399
  147.7 31.0 %collective-permute-start.56 = (bf16[192,1152]{1,0:T(8,128)(2,1)S(1)}, bf16[192,1152]{1,0:T(8,128)(2,1)S(1)}, u32[]{:S(2)}, u32[]{:S(2)}) collective-permute-start(bf16[192,1152]{1,0:T(8,128)(2,1)S(1)} %get-tuple-element.95), channel_id=1, source_target_pairs={{0,3},{1,2},{2,1},{3,0},{4,7},{5,6},{6,5},{7,4},{8,11},{9,10},{10,... | collective-permute-start | bytes 1327112 | tf_op jit(solution)/shard_map/ppermute | solution.py:399
  160.4 24.4 %collective-permute-start.51 = (bf16[192,1152]{1,0:T(8,128)(2,1)S(1)}, bf16[192,1152]{1,0:T(8,128)(2,1)S(1)}, u32[]{:S(2)}, u32[]{:S(2)}) collective-permute-start(bf16[192,1152]{1,0:T(8,128)(2,1)S(1)} %get-tuple-element.89), channel_id=1, source_target_pairs={{0,1},{1,0},{2,3},{3,2},{4,5},{5,4},{6,7},{7,6},{8,9},{9,8},{10,11... | collective-permute-start | bytes 1327112 | tf_op jit(solution)/shard_map/ppermute | solution.py:399
  160.7 24.1 %collective-permute-start.52 = (bf16[192,1152]{1,0:T(8,128)(2,1)S(1)}, bf16[192,1152]{1,0:T(8,128)(2,1)S(1)}, u32[]{:S(2)}, u32[]{:S(2)}) collective-permute-start(bf16[192,1152]{1,0:T(8,128)(2,1)S(1)} %get-tuple-element.90), channel_id=1, source_target_pairs={{0,8},{1,9},{2,10},{3,11},{4,12},{5,13},{6,14},{7,15},{8,0},{9,1},... | collective-permute-start | bytes 1327112 | tf_op jit(solution)/shard_map/ppermute | solution.py:399
  165.3 26.7 %collective-permute-start.53 = (bf16[192,1152]{1,0:T(8,128)(2,1)S(1)}, bf16[192,1152]{1,0:T(8,128)(2,1)S(1)}, u32[]{:S(2)}, u32[]{:S(2)}) collective-permute-start(bf16[192,1152]{1,0:T(8,128)(2,1)S(1)} %get-tuple-element.91), channel_id=1, source_target_pairs={{0,9},{1,8},{2,11},{3,10},{4,13},{5,12},{6,15},{7,14},{8,1},{9,0},... | collective-permute-start | bytes 1327112 | tf_op jit(solution)/shard_map/ppermute | solution.py:399
  197.4 19.0 %collective-permute-start.57 = (bf16[192,1152]{1,0:T(8,128)(2,1)S(1)}, bf16[192,1152]{1,0:T(8,128)(2,1)S(1)}, u32[]{:S(2)}, u32[]{:S(2)}) collective-permute-start(bf16[192,1152]{1,0:T(8,128)(2,1)S(1)} %last.1.refs_1_), channel_id=1, source_target_pairs={{0,1},{1,0},{2,3},{3,2},{4,5},{5,4},{6,7},{7,6},{8,9},{9,8},{10,11... | collective-permute-start | bytes 1327112 | tf_op jit(solution)/shard_map/ppermute | solution.py:391
  198.7 32.9 %collective-permute-start.58 = (bf16[192,1152]{1,0:T(8,128)(2,1)S(1)}, bf16[192,1152]{1,0:T(8,128)(2,1)S(1)}, u32[]{:S(2)}, u32[]{:S(2)}) collective-permute-start(bf16[192,1152]{1,0:T(8,128)(2,1)S(1)} %last.1.refs_1_), channel_id=1, source_target_pairs={{0,2},{1,3},{2,0},{3,1},{4,6},{5,7},{6,4},{7,5},{8,10},{9,11},{10,... | collective-permute-start | bytes 1327112 | tf_op jit(solution)/shard_map/ppermute | solution.py:391
  201.5 30.1 %collective-permute-start.59 = (bf16[192,1152]{1,0:T(8,128)(2,1)S(1)}, bf16[192,1152]{1,0:T(8,128)(2,1)S(1)}, u32[]{:S(2)}, u32[]{:S(2)}) collective-permute-start(bf16[192,1152]{1,0:T(8,128)(2,1)S(1)} %last.1.refs_1_), channel_id=1, source_target_pairs={{0,3},{1,2},{2,1},{3,0},{4,7},{5,6},{6,5},{7,4},{8,11},{9,10},{10,... | collective-permute-start | bytes 1327112 | tf_op jit(solution)/shard_map/ppermute | solution.py:391
  249.6 12.0 %collective-permute-start.66 = (bf16[144,1152]{1,0:T(8,128)(2,1)S(1)}, bf16[144,1152]{1,0:T(8,128)(2,1)S(1)}, u32[]{:S(2)}, u32[]{:S(2)}) collective-permute-start(bf16[144,1152]{1,0:T(8,128)(2,1)S(1)} %get-tuple-element.112), channel_id=1, source_target_pairs={{0,16},{4,20},{8,24},{12,28},{16,0},{20,4},{24,8},{28,12},{1,17},{... | collective-permute-start | bytes 995336 | tf_op jit(solution)/shard_map/ppermute | solution.py:387
  250.5 16.9 %collective-permute-start.67 = (bf16[144,1152]{1,0:T(8,128)(2,1)S(1)}, bf16[144,1152]{1,0:T(8,128)(2,1)S(1)}, u32[]{:S(2)}, u32[]{:S(2)}) collective-permute-start(bf16[144,1152]{1,0:T(8,128)(2,1)S(1)} %get-tuple-element.111), channel_id=1, source_target_pairs={{0,24},{4,28},{8,16},{12,20},{16,8},{20,12},{24,0},{28,4},{1,25},{... | collective-permute-start | bytes 995336 | tf_op jit(solution)/shard_map/ppermute | solution.py:387
  253.0 19.1 %collective-permute-start.62 = (bf16[144,1152]{1,0:T(8,128)(2,1)S(1)}, bf16[144,1152]{1,0:T(8,128)(2,1)S(1)}, u32[]{:S(2)}, u32[]{:S(2)}) collective-permute-start(bf16[144,1152]{1,0:T(8,128)(2,1)S(1)} %get-tuple-element.113), channel_id=1, source_target_pairs={{0,8},{4,12},{8,0},{12,4},{16,24},{20,28},{24,16},{28,20},{1,9},{5... | collective-permute-start | bytes 995336 | tf_op jit(solution)/shard_map/ppermute | solution.py:387
  254.6 20.0 %collective-permute-start.63 = (bf16[144,1152]{1,0:T(8,128)(2,1)S(1)}, bf16[144,1152]{1,0:T(8,128)(2,1)S(1)}, u32[]{:S(2)}, u32[]{:S(2)}) collective-permute-start(bf16[144,1152]{1,0:T(8,128)(2,1)S(1)} %get-tuple-element.115), channel_id=1, source_target_pairs={{0,16},{4,20},{8,24},{12,28},{16,0},{20,4},{24,8},{28,12},{1,17},{... | collective-permute-start | bytes 995336 | tf_op jit(solution)/shard_map/ppermute | solution.py:387
  259.8 20.6 %collective-permute-start.64 = (bf16[144,1152]{1,0:T(8,128)(2,1)S(1)}, bf16[144,1152]{1,0:T(8,128)(2,1)S(1)}, u32[]{:S(2)}, u32[]{:S(2)}) collective-permute-start(bf16[144,1152]{1,0:T(8,128)(2,1)S(1)} %get-tuple-element.114), channel_id=1, source_target_pairs={{0,24},{4,28},{8,16},{12,20},{16,8},{20,12},{24,0},{28,4},{1,25},{... | collective-permute-start | bytes 995336 | tf_op jit(solution)/shard_map/ppermute | solution.py:387
  (70 other events, 1054.9 us)
where the time goes:
time: 287 us; the launch traced here: 281 us
  waiting for transfers between devices  135 us (47%)
  starting transfers between devices  63.8 us (22%)
  Pallas kernels  57.5 us (20%)
  other arithmetic  11.5 us (4%)
  local copies, waits for them, and re-layouts  10.5 us (4%)
    ppermute x8, waiting for transfers between devices, swap_col(): lax.ppermute(value, 'col', [(spot, spot ^ flip) for spot in range(size)])  54.4 us
    ppermute x48, waiting for transfers between devices, swap_plane(): lax.ppermute(value, PLANE, [(spot, spot ^ flip) for spot in range(size)])  41 us
    ppermute x12, waiting for transfers between devices, swap_both(): return lax.ppermute(value, ('dp', 'row', 'col'), pairs)  39.7 us
    ppermute x48, starting transfers between devices, swap_plane(): lax.ppermute(value, PLANE, [(spot, spot ^ flip) for spot in range(size)])  39.2 us
    pallas_call x3, Pallas kernels, forward(): pl.pallas_call(functools.partial(forward_kernel, count, first_mod, save,...  34.7 us
    ppermute x12, starting transfers between devices, swap_both(): return lax.ppermute(value, ('dp', 'row', 'col'), pairs)  13.1 us
    ppermute x8, starting transfers between devices, swap_col(): lax.ppermute(value, 'col', [(spot, spot ^ flip) for spot in range(size)])  11.6 us
    pallas_call x2, Pallas kernels, weight_grad(): pl.pallas_call(functools.partial(weight_grad_kernel, len(backs), len(shap...  9.82 us
  transfers between devices with their start and end apart: 68, of which 29 were waited for; matrix products, arithmetic and copies ran while one was open for 6% of the time, Pallas kernels for 14%

commit v1 on v0

--- a/solution.py
+++ b/solution.py
@@ -41,14 +41,6 @@
     mixed = mixing(seeds * 1103515245 + places * 40503 + 12345)
     uniform = (lax.shift_right_logical(mixed, jnp.int32(8)).astype(F32) + 0.5) * (1.0 / 16777216.0)
     return math.sqrt(2.0) * lax.erf_inv(2.0 * uniform - 1.0)
-
-
-def column_tile(width, most=1152):
-    best = 128
-    for tile in range(128, most + 1, 128):
-        if width % tile == 0:
-            best = tile
-    return best
 
 
 def gelu(pre):
@@ -123,9 +115,12 @@
             base = dot(upright(state[group, sample]), patch[...], ((1,), (0,)))
             base = place(base, down_pos[group], across[...])
             normed, _ = layer_norm(base)
-            spot = (group // per_set) * samples + sample if per_set else sample
-            shift = mods[spot, pl.ds(first_mod, 1), :]
-            scale = mods[spot, pl.ds(first_mod + 1, 1), :]
+            spot = sample * 9 + first_mod
+            if per_set:
+                abroad = samples * 9 + sample * 4 + first_mod // 3 * 2
+                spot = jnp.where(group < per_set, spot, abroad)
+            shift = mods[pl.ds(spot, 1), :]
+            scale = mods[pl.ds(spot + 1, 1), :]
             row = pl.multiple_of((group * samples + sample) * tokens, tokens)
             act[pl.ds(row, tokens), :] = (normed * (1.0 + scale) + shift).astype(BF16)
         return carry
@@ -197,7 +192,8 @@
     mixed = parts[0][rows].astype(F32)
     for part in parts[1:]:
         mixed = mixed + part[rows].astype(F32)
-    gate = mods[sample, gate_at : gate_at + 1, :]
+    gate_row = sample * 9 + gate_at
+    gate = mods[gate_row : gate_row + 1, :]
     base = dot(upright(state[sample]), patch[...], ((1,), (0,)))
     base = place(base, down_pos[0], across[...])
     final, reciprocal = layer_norm(base + gate * mixed)
@@ -297,37 +293,45 @@
         copy.wait()
 
 
-def weight_grad_kernel(groups, outs, *refs):
+def gather_rows(parts, whole):
+    at = 0
+    for part in parts:
+        rows = part.shape[0]
+        whole[at : at + rows, :] = part[...]
+        at += rows
+
+
+def weight_grad_kernel(lefts, rights, start, more, outs, *refs):
     order, refs = refs[0], refs[1:]
-    backs, hidden, blocks = refs[:groups], refs[groups], refs[groups + 1 : groups + 1 + outs]
-    back, grad, sem = refs[groups + 1 + outs :]
-    rows = backs[0].shape[0]
-    for group in range(groups):
-        back[group * rows : (group + 1) * rows, :] = backs[group][...]
-    features = back.shape[1]
-    tile = column_tile(features)
-
-    def step(index, carry):
-        at = pl.multiple_of(index * tile, tile)
-        grad[pl.ds(at, tile), :] = dot(back[:, pl.ds(at, tile)], hidden[...], ((0,), (0,)))
-        return carry
-
-    lax.fori_loop(0, features // tile, step, 0)
-    store_blocks(order, grad, blocks, sem)
-
-
-def back_pre_kernel(groups, pieces, *refs):
+    left_parts, refs = refs[:lefts], refs[lefts:]
+    right_parts, refs = refs[:rights], refs[rights:]
+    so_far, refs = (refs[0], refs[1:]) if more else (None, refs)
+    blocks, (left, right, grad, sem) = refs[:-4], refs[-4:]
+    gather_rows(left_parts, left)
+    total = left.shape[0]
+    if rights == 1:
+        values = right_parts[0][start : start + total, :]
+    else:
+        gather_rows(right_parts, right)
+        values = right[...]
+    target = grad if outs else blocks[0]
+    part = dot(left[...], values, ((0,), (0,)))
+    target[...] = part + so_far[...] if more else part
+    if outs:
+        store_blocks(order, grad, blocks, sem)
+
+
+def back_pre_kernel(groups, pieces, start, *refs):
     order, refs = refs[0], refs[1:]
     backs, pre, refs = refs[:groups], refs[groups], refs[groups + 1 :]
-    down_pieces, back_pre, back, down, sem = refs[:pieces], *refs[pieces:]
+    down_pieces, (back_pre, back, down, sem) = refs[:pieces], refs[pieces:]
     copies = load_pieces(order, down_pieces, down, sem)
-    rows = backs[0].shape[0]
-    for group in range(groups):
-        back[group * rows : (group + 1) * rows, :] = backs[group][...]
+    gather_rows(backs, back)
     for copy in copies:
         copy.wait()
+    rows = back.shape[0]
     back_hidden = dot(back[...], down[...], ((1,), (0,)))
-    back_pre[...] = (back_hidden * gelu_slope(pre[...])).astype(BF16)
+    back_pre[...] = (back_hidden * gelu_slope(pre[start : start + rows, :])).astype(BF16)
 
 
 def block_shapes(count, features, width):
@@ -336,33 +340,38 @@
     return [jax.ShapeDtypeStruct((count // 2, features // count, width), F32)] * 2
 
 
-def weight_grad(order, backs, hidden, count):
-    features = backs[0].shape[1]
-    total, width = hidden.shape
-    shapes = block_shapes(count, features, width)
+def weight_grad(order, lefts, rights, count, start=0, so_far=None, whole=False):
+    features, width = lefts[0].shape[1], rights[0].shape[1]
+    total = sum(part.shape[0] for part in lefts)
+    shapes = [jax.ShapeDtypeStruct((features, width), F32)] if whole else block_shapes(count, features, width)
+    outs = 0 if whole else len(shapes)
+    more = [] if so_far is None else [so_far]
+    vmem = len(lefts) + len(rights) + len(more)
     return pl.pallas_call(
-        functools.partial(weight_grad_kernel, len(backs), len(shapes)),
+        functools.partial(weight_grad_kernel, len(lefts), len(rights), start, bool(more), outs),
         out_shape=shapes,
-        in_specs=[full(pltpu.SMEM)] + [full()] * (len(backs) + 1),
-        out_specs=[full(pltpu.HBM)] * len(shapes),
+        in_specs=[full(pltpu.SMEM)] + [full()] * vmem,
+        out_specs=[full() if whole else full(pl.ANY)] * len(shapes),
         scratch_shapes=[
             pltpu.VMEM((total, features), BF16),
-            pltpu.VMEM((features, width), F32),
+            pltpu.VMEM((total if len(rights) > 1 else 16, width), BF16),
+            pltpu.VMEM((8, width) if whole else (features, width), F32),
             pltpu.SemaphoreType.DMA((count,)),
         ],
         compiler_params=pltpu.CompilerParams(vmem_limit_bytes=VMEM_LIMIT),
         cost_estimate=pl.CostEstimate(
             flops=2 * total * features * width, bytes_accessed=8 * features * width, transcendentals=0
         ),
-    )(order, *backs, hidden)
-
-
-def back_through(order, backs, pre, down_pieces):
+    )(order, *lefts, *rights, *more)
+
+
+def back_through(order, backs, pre, down_pieces, start):
     features = backs[0].shape[1]
-    total, width = pre.shape
+    width = pre.shape[1]
+    total = sum(back.shape[0] for back in backs)
     pieces = len(down_pieces)
     return pl.pallas_call(
-        functools.partial(back_pre_kernel, len(backs), pieces),
+        functools.partial(back_pre_kernel, len(backs), pieces, start),
         out_shape=jax.ShapeDtypeStruct((total, width), BF16),
         in_specs=[full(pltpu.SMEM)] + [full()] * (len(backs) + 1) + [full(pltpu.HBM)] * pieces,
         out_specs=full(),
@@ -375,7 +384,6 @@
         cost_estimate=pl.CostEstimate(
             flops=2 * total * features * width, bytes_accessed=8 * features * width, transcendentals=total * width
         ),
-        name="back_pre",
     )(order, *backs, pre, *down_pieces)
 
 
@@ -468,15 +476,20 @@
 
 def modulation_columns(own, columns, col):
     sets, samples = own.shape[:2]
-    own = own.reshape(sets * samples, 9, own.shape[2] // 9)
-    gathered = spread_col(own, columns)
+    share = own.shape[2] // 9
+    rows = own.reshape(sets, samples, 9, share)
+    packed = [rows[0].reshape(samples * 9, share)]
+    for other in range(1, sets):
+        packed.append(jnp.concatenate([rows[other, :, 0:2], rows[other, :, 3:5]], axis=1).reshape(samples * 4, share))
+    packed = jnp.concatenate(packed, axis=0)
+    gathered = spread_col(packed, columns)
     ordered = []
     for place_at in range(columns):
         piece = gathered[place_at]
         for other in range(1, columns):
             piece = jnp.where(col == other, gathered[place_at ^ other], piece)
         ordered.append(piece)
-    return jnp.concatenate(ordered, axis=2)
+    return jnp.concatenate(ordered, axis=1)
 
 
 def positions(chunks, tokens):
@@ -551,8 +564,8 @@
     own_mods = modulation_sum(part, samples, fast, square, plane)
     mods = modulation_columns(own_mods, columns, col)
     teacher_up_pieces = cores(up_shards)
-    down_shards = chips(*after(teacher_shards(teacher_down, down_abroad), up_shards))
-    teacher_down_pieces = cores(after(down_shards, mods))
+    down_shards = chips(*teacher_shards(teacher_down, down_abroad))
+    teacher_down_pieces = cores(down_shards)
     student_down_shards = chips(after(student_down, own_mods))
     latents, seeds, col, step_index = after((latents, seeds, col, step_index), part)
 
@@ -594,6 +607,7 @@
             first_mod, False, 2 if square else 0,
         )
 
+    student_up_pieces = cores(after(student_up_shards, down_shards))
     teacher_pos, teacher_noisy = pos, noisy
     if square:
         near = noisy[:2]
@@ -602,14 +616,17 @@
     line = [(0, flip) for flip in range(columns)]
     parts = teach(teacher_noisy, 0)
     first = share(parts, members)
-    student_up_pieces = cores(after(student_up_shards, parts))
     student_down_pieces = cores(after(student_down_shards, parts))
     saved = forward(order, noisy, student_patch, pos, mods, student_up_pieces, student_down_pieces, 6, True)
     halfway = middle(coefs, noisy[0], teacher_patch, pos, mods, teacher_out, after(first, saved))
     half_all = jnp.stack([halfway] + [swap_both(halfway, flip, plane, columns) for flip in members[1:]], axis=0)
-    student_parts = after(saved[:columns], half_all)
+    early = swap_both(saved[2 % columns], line[2 % columns], plane, columns)
+    student = [saved[0], early] + [
+        swap_both(after(saved[spot], half_all), line[spot], plane, columns)
+        for spot in range(1, columns)
+        if spot != 2 % columns
+    ]
     second = share(teach(half_all, 3), members)
-    student = share(student_parts, line)
     act, pre, hidden = saved[columns:]
     back = last(
         coefs,
@@ -624,7 +641,12 @@
         second,
         student,
     )
-    backs = spread_col(back, columns)
+    if columns == 4:
+        across = swap_col(back, 2, columns)
+        beside = swap_col(back, 1, columns)
+        backs = [back, beside, across, swap_col(across, 1, columns)]
+    else:
+        backs = spread_col(back, columns)
 
     def pair_sum(blocks):
         if not fast:
@@ -640,12 +662,15 @@
             total = total + swap_plane(pair[flip].astype(BF16), 2 * flip, plane).astype(F32)
         return total
 
-    down_blocks = weight_grad(order, backs, hidden, count)
-    back_pre = back_through(order, backs, after(pre, down_blocks), student_down_pieces)
+    split = (columns - 1) * back.shape[0]
+    (down_early,) = weight_grad(order, backs[:-1], [hidden], count, whole=True)
+    pre_early = back_through(order, backs[:-1], pre, student_down_pieces, 0)
+    down_blocks = weight_grad(order, after(backs[-1:], pre_early), [hidden], count, split, down_early)
+    pre_late = back_through(order, backs[-1:], after(pre, down_blocks), student_down_pieces, split)
     down_pair = pair_sum(down_blocks)
-    up_blocks = weight_grad(order, [after(act, down_pair)], back_pre, count)
+    up_blocks = weight_grad(order, [after(act, down_pair)], [pre_early, pre_late], count)
+    down_gradient = chip_sum(down_pair)
     up_gradient = chip_sum(pair_sum(up_blocks))
-    down_gradient = chip_sum(down_pair)
     return (up_gradient, down_gradient)
 
 

time: 287 us -> 278 us (0.969); the launches traced: 281 us -> 277 us
  waiting for transfers between devices: 135 us -> 121 us
  starting transfers between devices: 63.8 us -> 70.7 us
    ppermute x8, waiting for transfers between devices: 54.4 us -> 29.2 us  [swap_col(): lax.ppermute(value, 'col', [(spot, spot ^ flip) for spot in range(size)])]
    ppermute x48, waiting for transfers between devices: 41 us -> 54.4 us  [swap_plane(): lax.ppermute(value, PLANE, [(spot, spot ^ flip) for spot in range(size)])]
    ppermute x48, starting transfers between devices: 39.2 us -> 43.6 us  [swap_plane(): lax.ppermute(value, PLANE, [(spot, spot ^ flip) for spot in range(size)])]
    pallas_call x3 -> x5, Pallas kernels: 15.3 us -> 18.5 us  [the longest x3 11.4 us: weight_grad(): pl.pallas_call(functools.partial(weight_grad_kernel, len(lefts), len(righ...]
    unnamed x70 -> x58, local copies, waits for them, and re-layouts: 6.09 us -> 5.09 us
  transfers between devices with their start and end apart: 68 -> 68, of which waited for: 29 -> 29; matrix products, arithmetic and copies ran while one was open for 6% -> 7% of each run, Pallas kernels for 14% -> 16%
where the time goes in v1:
time: 278 us; the launch traced here: 277 us
  waiting for transfers between devices  121 us (44%)
  starting transfers between devices  70.7 us (25%)
  Pallas kernels  58.9 us (21%)
  other arithmetic  13.6 us (5%)
  local copies, waits for them, and re-layouts  10 us (4%)
    ppermute x48, waiting for transfers between devices, swap_plane(): lax.ppermute(value, PLANE, [(spot, spot ^ flip) for spot in range(size)])  54.4 us
    ppermute x48, starting transfers between devices, swap_plane(): lax.ppermute(value, PLANE, [(spot, spot ^ flip) for spot in range(size)])  43.6 us
    ppermute x12, waiting for transfers between devices, swap_both(): return lax.ppermute(value, ('dp', 'row', 'col'), pairs)  37.3 us
    pallas_call x3, Pallas kernels, forward(): pl.pallas_call(functools.partial(forward_kernel, count, first_mod, save,...  32.9 us
    ppermute x8, waiting for transfers between devices, swap_col(): lax.ppermute(value, 'col', [(spot, spot ^ flip) for spot in range(size)])  29.2 us
    ppermute x12, starting transfers between devices, swap_both(): return lax.ppermute(value, ('dp', 'row', 'col'), pairs)  15.5 us
    ppermute x8, starting transfers between devices, swap_col(): lax.ppermute(value, 'col', [(spot, spot ^ flip) for spot in range(size)])  11.7 us
    pallas_call x3, Pallas kernels, weight_grad(): pl.pallas_call(functools.partial(weight_grad_kernel, len(lefts), len(righ...  11.4 us
  transfers between devices with their start and end apart: 68, of which 29 were waited for; matrix products, arithmetic and copies ran while one was open for 7% of the time, Pallas kernels for 16%

profile of v1, /device:TPU:0, one launch (start us, length us, event | category | flops | bytes accessed | tf_op | source)
XLA Modules:
  0.0 277.1 jit_solution(10570721125445555126)
XLA Ops:
  1.5 3.4 %collective-permute-start.6 = (s32[3]{0:T(128)S(1)}, s32[3]{0:T(128)S(1)}, u32[]{:S(2)}, u32[]{:S(2)}) collective-permute-start(s32[3]{0:T(128)S(1)} %multiply_add_fusion.1), channel_id=1, source_target_pairs={{0,28},{4,24},{8,20},{12,16},{16,12},{20,8},{24,4},{28,0},{1,29},{... | collective-permute-start | bytes 44 | tf_op jit(solution)/shard_map/ppermute | solution.py:395
  7.2 2.8 %collective-permute-start.7 = (bf16[144,1152]{1,0:T(8,128)(2,1)}, bf16[144,1152]{1,0:T(8,128)(2,1)}, u32[]{:S(2)}, u32[]{:S(2)}) collective-permute-start(bf16[144,1152]{1,0:T(8,128)(2,1)} %param.22), channel_id=1, source_target_pairs={{0,2},{1,3},{2,0},{3,1},{4,6},{5,7},{6,4},{7,5},{8,10},{9,11},{10,... | collective-permute-start | bytes 995336 | tf_op jit(solution)/shard_map/ppermute | solution.py:399
  21.7 3.6 %collective-permute-done.7 = bf16[144,1152]{1,0:T(8,128)(2,1)} collective-permute-done((bf16[144,1152]{1,0:T(8,128)(2,1)}, bf16[144,1152]{1,0:T(8,128)(2,1)}, u32[]{:S(2)}, u32[]{:S(2)}) %collective-permute-start.7) | collective-permute-done | bytes 331808 | tf_op jit(solution)/shard_map/ppermute | solution.py:399
  36.3 3.2 %collective-permute-start.17 = (bf16[144,1152]{1,0:T(8,128)(2,1)S(1)}, bf16[144,1152]{1,0:T(8,128)(2,1)S(1)}, u32[]{:S(2)}, u32[]{:S(2)}) collective-permute-start(bf16[144,1152]{1,0:T(8,128)(2,1)S(1)} %copy-done.3), channel_id=1, source_target_pairs={{0,24},{4,28},{8,16},{12,20},{16,8},{20,12},{24,0},{28,4},{1,25},{... | collective-permute-start | bytes 995336 | tf_op jit(solution)/shard_map/ppermute | solution.py:395
  39.5 8.1 %collective-permute-done.9 = f32[2,3,2592]{2,1,0:T(4,128)S(1)} collective-permute-done((f32[2,3,2592]{2,1,0:T(4,128)S(1)}, f32[2,3,2592]{2,1,0:T(4,128)S(1)}, u32[]{:S(2)}, u32[]{:S(2)}) %collective-permute-start.9) | collective-permute-done | bytes 62240 | tf_op jit(solution)/shard_map/ppermute | solution.py:395
  49.5 3.4 %collective-permute-start.13 = (f32[39,288]{1,0:T(8,128)S(1)}, f32[39,288]{1,0:T(8,128)S(1)}, u32[]{:S(2)}, u32[]{:S(2)}) collective-permute-start(f32[39,288]{1,0:T(8,128)S(1)} %pad_maximum_fusion.5), channel_id=1, source_target_pairs={{0,2},{1,3},{2,0},{3,1},{4,6},{5,7},{6,4},{7,5},{8,10},{9,11},{10,... | collective-permute-start | bytes 134792 | tf_op jit(solution)/shard_map/ppermute | solution.py:399
  56.7 4.4 %collective-permute-done.13 = f32[39,288]{1,0:T(8,128)S(1)} collective-permute-done((f32[39,288]{1,0:T(8,128)S(1)}, f32[39,288]{1,0:T(8,128)S(1)}, u32[]{:S(2)}, u32[]{:S(2)}) %collective-permute-start.13) | collective-permute-done | bytes 44960 | tf_op jit(solution)/shard_map/ppermute | solution.py:399
  67.4 4.2 %collective-permute-done.31.refs_8_ = bf16[144,1152]{1,0:T(8,128)(2,1)} collective-permute-done((bf16[144,1152]{1,0:T(8,128)(2,1)}, bf16[144,1152]{1,0:T(8,128)(2,1)}, u32[]{:S(2)}, u32[]{:S(2)}) %collective-permute-start.31) | collective-permute-done | bytes 331808 | tf_op jit(solution)/shard_map/ppermute | solution.py:395
  75.3 3.5 %collective-permute-done.28.refs_20_.refs_11_.refs_9_ = bf16[144,1152]{1,0:T(8,128)(2,1)S(1)} collective-permute-done((bf16[144,1152]{1,0:T(8,128)(2,1)S(1)}, bf16[144,1152]{1,0:T(8,128)(2,1)S(1)}, u32[]{:S(2)}, u32[]{:S(2)}) %collective-permute-start.28) | collective-permute-done | bytes 331808 | tf_op jit(solution)/shard_map/ppermute | solution.py:395
  80.9 5.0 %collective-permute-done.21.refs_20_ = bf16[144,1152]{1,0:T(8,128)(2,1)} collective-permute-done((bf16[144,1152]{1,0:T(8,128)(2,1)}, bf16[144,1152]{1,0:T(8,128)(2,1)}, u32[]{:S(2)}, u32[]{:S(2)}) %collective-permute-start.21) | collective-permute-done | bytes 331808 | tf_op jit(solution)/shard_map/ppermute | solution.py:395
  86.0 5.2 %collective-permute-done.19.refs_16_ = bf16[144,1152]{1,0:T(8,128)(2,1)} collective-permute-done((bf16[144,1152]{1,0:T(8,128)(2,1)}, bf16[144,1152]{1,0:T(8,128)(2,1)}, u32[]{:S(2)}, u32[]{:S(2)}) %collective-permute-start.19) | collective-permute-done | bytes 331808 | tf_op jit(solution)/shard_map/ppermute | solution.py:395
  99.5 10.6 %shard_map.158 = (bf16[192,1152]{1,0:T(8,128)(2,1)S(1)}, bf16[192,1152]{1,0:T(8,128)(2,1)S(1)}, bf16[192,1152]{1,0:T(8,128)(2,1)S(1)}, bf16[192,1152]{1,0:T(8,128)(2,1)S(1)}) custom-call(s32[8]{0:T(128)S(1)} %xor_multiply_fusion.refs_0_, f32[4,3,16,64]{3,2,1,0:T(8,128)S(1)} %pad_maximum_fusion.refs_1_, bf16[16,1152]{1,0:T(8,128)(2,1)S(1)} %copy-done.11, ...), custom_call_target="tpu_custom_call" | custom-call | flops 4076863488 | bytes 10616832 | tf_op jit(solution)/shard_map/pallas_call | solution.py:176
  116.2 11.8 %shard_map.159 = (bf16[192,1152]{1,0:T(8,128)(2,1)S(1)}, bf16[192,1152]{1,0:T(8,128)(2,1)S(1)}, bf16[192,1152]{1,0:T(8,128)(2,1)S(1)}, bf16[192,1152]{1,0:T(8,12...) custom-call(s32[8]{0:T(128)S(1)} %xor_multiply_fusion.refs_0_, ...), custom_call_target="tpu_custom_call" | custom-call | flops 4076863488 | bytes 10616832 | tf_op jit(solution)/shard_map/pallas_call | solution.py:176
  128.0 6.2 %collective-permute-done.46.refs_9_ = bf16[192,1152]{1,0:T(8,128)(2,1)S(1)} collective-permute-done((bf16[192,1152]{1,0:T(8,128)(2,1)S(1)}, bf16[192,1152]{1,0:T(8,128)(2,1)S(1)}, u32[]{:S(2)}, u32[]{:S(2)}) %collective-permute-start.46) | collective-permute-done | bytes 442400 | tf_op jit(solution)/shard_map/ppermute | solution.py:407
  139.9 3.3 %collective-permute-start.54 = (bf16[192,1152]{1,0:T(8,128)(2,1)S(1)}, bf16[192,1152]{1,0:T(8,128)(2,1)S(1)}, u32[]{:S(2)}, u32[]{:S(2)}) collective-permute-start(bf16[192,1152]{1,0:T(8,128)(2,1)S(1)} %get-tuple-element.67), channel_id=1, source_target_pairs={{0,2},{1,3},{2,0},{3,1},{4,6},{5,7},{6,4},{7,5},{8,10},{9,11},{10,... | collective-permute-start | bytes 1327112 | tf_op jit(solution)/shard_map/ppermute | solution.py:407
  144.1 3.5 %collective-permute-start.56 = (bf16[192,1152]{1,0:T(8,128)(2,1)S(1)}, bf16[192,1152]{1,0:T(8,128)(2,1)S(1)}, u32[]{:S(2)}, u32[]{:S(2)}) collective-permute-start(bf16[192,1152]{1,0:T(8,128)(2,1)S(1)} %get-tuple-element.80), channel_id=1, source_target_pairs={{0,3},{1,2},{2,1},{3,0},{4,7},{5,6},{6,5},{7,4},{8,11},{9,10},{10,... | collective-permute-start | bytes 1327112 | tf_op jit(solution)/shard_map/ppermute | solution.py:407
  147.6 10.6 %shard_map.160 = (bf16[192,1152]{1,0:T(8,128)(2,1)S(1)}, bf16[192,1152]{1,0:T(8,128)(2,1)S(1)}, bf16[192,1152]{1,0:T(8,128)(2,1)S(1)}, bf16[192,1152]{1,0:T(8,128)(2,1)S(1)}) custom-call(s32[8]{0:T(128)S(1)} %xor_multiply_fusion.refs_0_, f32[4,3,16,64]{3,2,1,0:T(8,128)S(1)} %pad_maximum_fusion.1.refs_1_, bf16[16,1152]{1,0:T(8,128)(2,1)S(1)} %copy-done.11, ...), custom_call_target="tpu_custom_call" | custom-call | flops 4076863488 | bytes 10616832 | tf_op jit(solution)/shard_map/pallas_call | solution.py:176
  159.3 4.8 %collective-permute-done.54.refs_15_ = bf16[192,1152]{1,0:T(8,128)(2,1)S(1)} collective-permute-done((bf16[192,1152]{1,0:T(8,128)(2,1)S(1)}, bf16[192,1152]{1,0:T(8,128)(2,1)S(1)}, u32[]{:S(2)}, u32[]{:S(2)}) %collective-permute-start.54) | collective-permute-done | bytes 442400 | tf_op jit(solution)/shard_map/ppermute | solution.py:407
  164.2 6.4 %collective-permute-done.55.refs_16_ = bf16[192,1152]{1,0:T(8,128)(2,1)S(1)} collective-permute-done((bf16[192,1152]{1,0:T(8,128)(2,1)S(1)}, bf16[192,1152]{1,0:T(8,128)(2,1)S(1)}, u32[]{:S(2)}, u32[]{:S(2)}) %collective-permute-start.55) | collective-permute-done | bytes 442400 | tf_op jit(solution)/shard_map/ppermute | solution.py:407
  170.6 3.3 %collective-permute-done.56.refs_17_ = bf16[192,1152]{1,0:T(8,128)(2,1)S(1)} collective-permute-done((bf16[192,1152]{1,0:T(8,128)(2,1)S(1)}, bf16[192,1152]{1,0:T(8,128)(2,1)S(1)}, u32[]{:S(2)}, u32[]{:S(2)}) %collective-permute-start.56) | collective-permute-done | bytes 442400 | tf_op jit(solution)/shard_map/ppermute | solution.py:407
  173.9 8.3 %collective-permute-done.51.refs_11_ = bf16[192,1152]{1,0:T(8,128)(2,1)S(1)} collective-permute-done((bf16[192,1152]{1,0:T(8,128)(2,1)S(1)}, bf16[192,1152]{1,0:T(8,128)(2,1)S(1)}, u32[]{:S(2)}, u32[]{:S(2)}) %collective-permute-start.51) | collective-permute-done | bytes 442400 | tf_op jit(solution)/shard_map/ppermute | solution.py:407
  182.3 7.9 %collective-permute-done.53.refs_13_ = bf16[192,1152]{1,0:T(8,128)(2,1)S(1)} collective-permute-done((bf16[192,1152]{1,0:T(8,128)(2,1)S(1)}, bf16[192,1152]{1,0:T(8,128)(2,1)S(1)}, u32[]{:S(2)}, u32[]{:S(2)}) %collective-permute-start.53) | collective-permute-done | bytes 442400 | tf_op jit(solution)/shard_map/ppermute | solution.py:407
  190.2 5.3 %last.1.refs_1_ = bf16[192,1152]{1,0:T(8,128)(2,1)S(1)} custom-call(f32[3,9]{1,0:T(4,128)S(1)} %select_select_fusion.4.refs_0_, f32[3,16,64]{2,1,0:T(8,128)S(1)} %slice_bitcast_fusion.10.refs_1_, f32[3,16,64]{2,1,0:T(8,128)S(1)} %middle.1.refs_2_, bf16[16,1152]{1,0:T(8,128)(2,1)S(1)} %copy-done.11, bf16[16,1152]{1,0:T(8,128)(2,1)S(1)} %copy-done.10, ...), custom_call_target="tpu_custom_call" | custom-call | flops 2000000000 | bytes 4000000 | tf_op jit(solution)/shard_map/last/pallas_call | solution.py:268
  199.9 17.7 %collective-permute-done.57.refs_3_ = bf16[192,1152]{1,0:T(8,128)(2,1)S(1)} collective-permute-done((bf16[192,1152]{1,0:T(8,128)(2,1)S(1)}, bf16[192,1152]{1,0:T(8,128)(2,1)S(1)}, u32[]{:S(2)}, u32[]{:S(2)}) %collective-permute-start.57) | collective-permute-done | bytes 442400 | tf_op jit(solution)/shard_map/ppermute | solution.py:399
  217.7 4.3 %shard_map.161.refs_2_ = bf16[576,1152]{1,0:T(8,128)(2,1)S(1)} custom-call(s32[8]{0:T(128)S(1)} %xor_multiply_fusion.refs_0_, bf16[192,1152]{1,0:T(8,128)(2,1)S(1)} %last.1.refs_1_, bf16[192,1152]{1,0:T(8,128)(2,1)S(1)} %collective-permute-done.59.refs_2_, bf16[192,1152]{1,0:T(8,128)(2,1)S(1)} %collective-permute-done.57.refs_3_, ...), custom_call_target="tpu_custom_call" | custom-call | flops 1528823808 | bytes 10616832 | tf_op jit(solution)/shard_map/pallas_call | solution.py:373
  222.0 3.1 %shard_map.162.refs_3_ = f32[1152,1152]{1,0:T(8,128)S(1)} custom-call(s32[8]{0:T(128)S(1)} %xor_multiply_fusion.refs_0_, bf16[192,1152]{1,0:T(8,128)(2,1)S(1)} %last.1.refs_1_, bf16[192,1152]{1,0:T(8,128)(2,1)S(1)} %collective-permute-done.59.refs_2_, bf16[192,1152]{1,0:T(8,128)(2,1)S(1)} %collective-permute-done.57.refs_3_, ...), custom_call_target="tpu_custom_call" | custom-call | flops 1528823808 | bytes 10616832 | tf_op jit(solution)/shard_map/pallas_call | solution.py:350
  225.1 3.3 %collective-permute-done.58.refs_1_ = bf16[192,1152]{1,0:T(8,128)(2,1)S(1)} collective-permute-done((bf16[192,1152]{1,0:T(8,128)(2,1)S(1)}, bf16[192,1152]{1,0:T(8,128)(2,1)S(1)}, u32[]{:S(2)}, u32[]{:S(2)}) %collective-permute-start.58) | collective-permute-done | bytes 442400 | tf_op jit(solution)/shard_map/ppermute | solution.py:399
  228.4 3.4 %shard_map.163 = (f32[4,144,1152]{2,1,0:T(8,128)S(1)}, f32[4,144,1152]{2,1,0:T(8,128)S(1)}) custom-call(s32[8]{0:T(128)S(1)} %xor_multiply_fusion.refs_0_, bf16[192,1152]{1,0:T(8,128)(2,1)S(1)} %collective-permute-done.58.refs_1_, bf16[768,1152]{1,0:T(8,128)(2,1)S(1)} %get-tuple-element.70.refs_4_.refs_2_, f32[1152,1152]{1,0:T(8,128)S(1)} %shard_map.162.refs_3_), custom_call_target="tpu_custom_call" | custom-call | flops 509607936 | bytes 10616832 | tf_op jit(solution)/shard_map/pallas_call | solution.py:350
  231.8 2.8 %shard_map.164.refs_3_ = bf16[192,1152]{1,0:T(8,128)(2,1)S(1)} custom-call(s32[8]{0:T(128)S(1)} %xor_multiply_fusion.refs_0_, bf16[192,1152]{1,0:T(8,128)(2,1)S(1)} %collective-permute-done.58.refs_1_, f32[768,1152]{1,0:T(8,128)S(1)} %get-tuple-element.85.refs_4_.refs_2_, bf16[144,1152]{1,0:T(8,128)(2,1)S(1)} %copy-done.2, ...), custom_call_target="tpu_custom_call" | custom-call | flops 509607936 | bytes 10616832 | tf_op jit(solution)/shard_map/pallas_call | solution.py:373
  237.1 5.0 %shard_map.165 = (f32[4,144,1152]{2,1,0:T(8,128)S(1)}, f32[4,144,1152]{2,1,0:T(8,128)S(1)}) custom-call(s32[8]{0:T(128)S(1)} %xor_multiply_fusion.refs_0_, bf16[768,1152]{1,0:T(8,128)(2,1)S(1)} %get-tuple-element.84.refs_1_, bf16[576,1152]{1,0:T(8,128)(2,1)S(1)} %shard_map.161.refs_2_, bf16[192,1152]{1,0:T(8,128)(2,1)S(1)} %shard_map.164.refs_3_), custom_call_target="tpu_custom_call" | custom-call | flops 2038431744 | bytes 10616832 | tf_op jit(solution)/shard_map/pallas_call | solution.py:350
  250.8 10.1 %collective-permute-done.65 = bf16[144,1152]{1,0:T(8,128)(2,1)S(1)} collective-permute-done((bf16[144,1152]{1,0:T(8,128)(2,1)S(1)}, bf16[144,1152]{1,0:T(8,128)(2,1)S(1)}, u32[]{:S(2)}, u32[]{:S(2)}) %collective-permute-start.65) | collective-permute-done | bytes 331808 | tf_op jit(solution)/shard_map/ppermute | solution.py:395
  263.4 11.3 %collective-permute-done.62 = bf16[144,1152]{1,0:T(8,128)(2,1)S(1)} collective-permute-done((bf16[144,1152]{1,0:T(8,128)(2,1)S(1)}, bf16[144,1152]{1,0:T(8,128)(2,1)S(1)}, u32[]{:S(2)}, u32[]{:S(2)}) %collective-permute-start.62) | collective-permute-done | bytes 331808 | tf_op jit(solution)/shard_map/ppermute | solution.py:395
  (245 shorter events, 86.1 us)
Async XLA Ops:
  1.5 15.2 %collective-permute-start.6 = (s32[3]{0:T(128)S(1)}, s32[3]{0:T(128)S(1)}, u32[]{:S(2)}, u32[]{:S(2)}) collective-permute-start(s32[3]{0:T(128)S(1)} %multiply_add_fusion.1), channel_id=1, source_target_pairs={{0,28},{4,24},{8,20},{12,16},{16,12},{20,8},{24,4},{28,0},{1,29},{... | collective-permute-start | bytes 44 | tf_op jit(solution)/shard_map/ppermute | solution.py:395
  7.2 18.1 %collective-permute-start.7 = (bf16[144,1152]{1,0:T(8,128)(2,1)}, bf16[144,1152]{1,0:T(8,128)(2,1)}, u32[]{:S(2)}, u32[]{:S(2)}) collective-permute-start(bf16[144,1152]{1,0:T(8,128)(2,1)} %param.22), channel_id=1, source_target_pairs={{0,2},{1,3},{2,0},{3,1},{4,6},{5,7},{6,4},{7,5},{8,10},{9,11},{10,... | collective-permute-start | bytes 995336 | tf_op jit(solution)/shard_map/ppermute | solution.py:399
  18.6 30.1 %collective-permute-start.16 = (bf16[144,1152]{1,0:T(8,128)(2,1)S(1)}, bf16[144,1152]{1,0:T(8,128)(2,1)S(1)}, u32[]{:S(2)}, u32[]{:S(2)}) collective-permute-start(bf16[144,1152]{1,0:T(8,128)(2,1)S(1)} %copy-done.3), channel_id=1, source_target_pairs={{0,16},{4,20},{8,24},{12,28},{16,0},{20,4},{24,8},{28,12},{1,17},{... | collective-permute-start | bytes 995336 | tf_op jit(solution)/shard_map/ppermute | solution.py:395
  20.1 29.4 %collective-permute-start.15 = (bf16[144,1152]{1,0:T(8,128)(2,1)S(1)}, bf16[144,1152]{1,0:T(8,128)(2,1)}, u32[]{:S(2)}, u32[]{:S(2)}) collective-permute-start(bf16[144,1152]{1,0:T(8,128)(2,1)S(1)} %copy-done.3), channel_id=1, source_target_pairs={{0,8},{4,12},{8,0},{12,4},{16,24},{20,28},{24,16},{28,20},{1,9},{5... | collective-permute-start | bytes 995336 | tf_op jit(solution)/shard_map/ppermute | solution.py:395
  36.3 16.6 %collective-permute-start.17 = (bf16[144,1152]{1,0:T(8,128)(2,1)S(1)}, bf16[144,1152]{1,0:T(8,128)(2,1)S(1)}, u32[]{:S(2)}, u32[]{:S(2)}) collective-permute-start(bf16[144,1152]{1,0:T(8,128)(2,1)S(1)} %copy-done.3), channel_id=1, source_target_pairs={{0,24},{4,28},{8,16},{12,20},{16,8},{20,12},{24,0},{28,4},{1,25},{... | collective-permute-start | bytes 995336 | tf_op jit(solution)/shard_map/ppermute | solution.py:395
  39.5 23.0 %collective-permute-start.18 = (bf16[144,1152]{1,0:T(8,128)(2,1)}, bf16[144,1152]{1,0:T(8,128)(2,1)}, u32[]{:S(2)}, u32[]{:S(2)}) collective-permute-start(bf16[144,1152]{1,0:T(8,128)(2,1)} %param.23), channel_id=1, source_target_pairs={{0,2},{1,3},{2,0},{3,1},{4,6},{5,7},{6,4},{7,5},{8,10},{9,11},{10,... | collective-permute-start | bytes 995336 | tf_op jit(solution)/shard_map/ppermute | solution.py:399
  55.5 16.1 %collective-permute-start.31 = (bf16[144,1152]{1,0:T(8,128)(2,1)}, bf16[144,1152]{1,0:T(8,128)(2,1)}, u32[]{:S(2)}, u32[]{:S(2)}) collective-permute-start(bf16[144,1152]{1,0:T(8,128)(2,1)} %get-tuple-element.104), channel_id=1, source_target_pairs={{0,8},{4,12},{8,0},{12,4},{16,24},{20,28},{24,16},{28,20},{1,9},{5... | collective-permute-start | bytes 995336 | tf_op jit(solution)/shard_map/ppermute | solution.py:395
  62.5 16.3 %collective-permute-start.28 = (bf16[144,1152]{1,0:T(8,128)(2,1)S(1)}, bf16[144,1152]{1,0:T(8,128)(2,1)S(1)}, u32[]{:S(2)}, u32[]{:S(2)}) collective-permute-start(bf16[144,1152]{1,0:T(8,128)(2,1)S(1)} %copy-done.2), channel_id=1, source_target_pairs={{0,24},{4,28},{8,16},{12,20},{16,8},{20,12},{24,0},{28,4},{1,25},{... | collective-permute-start | bytes 995336 | tf_op jit(solution)/shard_map/ppermute | solution.py:395
  65.1 20.8 %collective-permute-start.21 = (bf16[144,1152]{1,0:T(8,128)(2,1)}, bf16[144,1152]{1,0:T(8,128)(2,1)}, u32[]{:S(2)}, u32[]{:S(2)}) collective-permute-start(bf16[144,1152]{1,0:T(8,128)(2,1)} %get-tuple-element.102), channel_id=1, source_target_pairs={{0,24},{4,28},{8,16},{12,20},{16,8},{20,12},{24,0},{28,4},{1,25},{... | collective-permute-start | bytes 995336 | tf_op jit(solution)/shard_map/ppermute | solution.py:395
  71.6 19.5 %collective-permute-start.19 = (bf16[144,1152]{1,0:T(8,128)(2,1)}, bf16[144,1152]{1,0:T(8,128)(2,1)}, u32[]{:S(2)}, u32[]{:S(2)}) collective-permute-start(bf16[144,1152]{1,0:T(8,128)(2,1)} %get-tuple-element.102), channel_id=1, source_target_pairs={{0,8},{4,12},{8,0},{12,4},{16,24},{20,28},{24,16},{28,20},{1,9},{5... | collective-permute-start | bytes 995336 | tf_op jit(solution)/shard_map/ppermute | solution.py:395
  73.2 17.9 %collective-permute-start.20 = (bf16[144,1152]{1,0:T(8,128)(2,1)S(1)}, bf16[144,1152]{1,0:T(8,128)(2,1)}, u32[]{:S(2)}, u32[]{:S(2)}) collective-permute-start(bf16[144,1152]{1,0:T(8,128)(2,1)S(1)} %get-tuple-element.103.refs_14_), channel_id=1, source_target_pairs={{0,16},{4,20},{8,24},{12,28},{16,0},{20,4},{24,8},{28,12},{1,17},{... | collective-permute-start | bytes 995336 | tf_op jit(solution)/shard_map/ppermute | solution.py:395
  79.3 15.9 %collective-permute-start.37 = (bf16[144,1152]{1,0:T(8,128)(2,1)S(1)}, bf16[144,1152]{1,0:T(8,128)(2,1)}, u32[]{:S(2)}, u32[]{:S(2)}) collective-permute-start(bf16[144,1152]{1,0:T(8,128)(2,1)S(1)} %get-tuple-element.103.refs_14_), channel_id=1, source_target_pairs={{0,4},{4,0},{8,12},{12,8},{16,20},{20,16},{24,28},{28,24},{1,5},{5... | collective-permute-start | bytes 995336 | tf_op jit(solution)/shard_map/ppermute | solution.py:395
  94.3 15.8 %collective-permute-start.27 = (bf16[144,1152]{1,0:T(8,128)(2,1)S(1)}, bf16[144,1152]{1,0:T(8,128)(2,1)S(1)}, u32[]{:S(2)}, u32[]{:S(2)}) collective-permute-start(bf16[144,1152]{1,0:T(8,128)(2,1)S(1)} %copy-done.2), channel_id=1, source_target_pairs={{0,16},{4,20},{8,24},{12,28},{16,0},{20,4},{24,8},{28,12},{1,17},{... | collective-permute-start | bytes 995336 | tf_op jit(solution)/shard_map/ppermute | solution.py:395
  95.2 15.4 %collective-permute-start.26 = (bf16[144,1152]{1,0:T(8,128)(2,1)S(1)}, bf16[144,1152]{1,0:T(8,128)(2,1)S(1)}, u32[]{:S(2)}, u32[]{:S(2)}) collective-permute-start(bf16[144,1152]{1,0:T(8,128)(2,1)S(1)} %copy-done.2), channel_id=1, source_target_pairs={{0,8},{4,12},{8,0},{12,4},{16,24},{20,28},{24,16},{28,20},{1,9},{5... | collective-permute-start | bytes 995336 | tf_op jit(solution)/shard_map/ppermute | solution.py:395
  97.0 14.1 %collective-permute-start.23 = (bf16[144,1152]{1,0:T(8,128)(2,1)}, bf16[144,1152]{1,0:T(8,128)(2,1)S(1)}, u32[]{:S(2)}, u32[]{:S(2)}) collective-permute-start(bf16[144,1152]{1,0:T(8,128)(2,1)} %collective-permute-done.15.refs_8_), channel_id=1, source_target_pairs={{0,4},{4,0},{8,12},{12,8},{16,20},{20,16},{24,28},{28,24},{1,5},{5... | collective-permute-start | bytes 995336 | tf_op jit(solution)/shard_map/ppermute | solution.py:395
  111.8 16.2 %collective-permute-start.45 = (bf16[192,1152]{1,0:T(8,128)(2,1)S(1)}, bf16[192,1152]{1,0:T(8,128)(2,1)S(1)}, u32[]{:S(2)}, u32[]{:S(2)}) collective-permute-start(bf16[192,1152]{1,0:T(8,128)(2,1)S(1)} %get-tuple-element.57), channel_id=1, source_target_pairs={{0,1},{1,0},{2,3},{3,2},{4,5},{5,4},{6,7},{7,6},{8,9},{9,8},{10,11... | collective-permute-start | bytes 1327112 | tf_op jit(solution)/shard_map/ppermute | solution.py:407
  112.4 21.8 %collective-permute-start.46 = (bf16[192,1152]{1,0:T(8,128)(2,1)S(1)}, bf16[192,1152]{1,0:T(8,128)(2,1)S(1)}, u32[]{:S(2)}, u32[]{:S(2)}) collective-permute-start(bf16[192,1152]{1,0:T(8,128)(2,1)S(1)} %get-tuple-element.58), channel_id=1, source_target_pairs={{0,8},{1,9},{2,10},{3,11},{4,12},{5,13},{6,14},{7,15},{8,0},{9,1},... | collective-permute-start | bytes 1327112 | tf_op jit(solution)/shard_map/ppermute | solution.py:407
  112.8 21.5 %collective-permute-start.47 = (bf16[192,1152]{1,0:T(8,128)(2,1)S(1)}, bf16[192,1152]{1,0:T(8,128)(2,1)S(1)}, u32[]{:S(2)}, u32[]{:S(2)}) collective-permute-start(bf16[192,1152]{1,0:T(8,128)(2,1)S(1)} %get-tuple-element.59), channel_id=1, source_target_pairs={{0,9},{1,8},{2,11},{3,10},{4,13},{5,12},{6,15},{7,14},{8,1},{9,0},... | collective-permute-start | bytes 1327112 | tf_op jit(solution)/shard_map/ppermute | solution.py:407
  139.9 24.2 %collective-permute-start.54 = (bf16[192,1152]{1,0:T(8,128)(2,1)S(1)}, bf16[192,1152]{1,0:T(8,128)(2,1)S(1)}, u32[]{:S(2)}, u32[]{:S(2)}) collective-permute-start(bf16[192,1152]{1,0:T(8,128)(2,1)S(1)} %get-tuple-element.67), channel_id=1, source_target_pairs={{0,2},{1,3},{2,0},{3,1},{4,6},{5,7},{6,4},{7,5},{8,10},{9,11},{10,... | collective-permute-start | bytes 1327112 | tf_op jit(solution)/shard_map/ppermute | solution.py:407
  143.6 27.0 %collective-permute-start.55 = (bf16[192,1152]{1,0:T(8,128)(2,1)S(1)}, bf16[192,1152]{1,0:T(8,128)(2,1)S(1)}, u32[]{:S(2)}, u32[]{:S(2)}) collective-permute-start(bf16[192,1152]{1,0:T(8,128)(2,1)S(1)} %get-tuple-element.79), channel_id=1, source_target_pairs={{0,1},{1,0},{2,3},{3,2},{4,5},{5,4},{6,7},{7,6},{8,9},{9,8},{10,11... | collective-permute-start | bytes 1327112 | tf_op jit(solution)/shard_map/ppermute | solution.py:407
  144.1 29.9 %collective-permute-start.56 = (bf16[192,1152]{1,0:T(8,128)(2,1)S(1)}, bf16[192,1152]{1,0:T(8,128)(2,1)S(1)}, u32[]{:S(2)}, u32[]{:S(2)}) collective-permute-start(bf16[192,1152]{1,0:T(8,128)(2,1)S(1)} %get-tuple-element.80), channel_id=1, source_target_pairs={{0,3},{1,2},{2,1},{3,0},{4,7},{5,6},{6,5},{7,4},{8,11},{9,10},{10,... | collective-permute-start | bytes 1327112 | tf_op jit(solution)/shard_map/ppermute | solution.py:407
  158.2 24.1 %collective-permute-start.51 = (bf16[192,1152]{1,0:T(8,128)(2,1)S(1)}, bf16[192,1152]{1,0:T(8,128)(2,1)S(1)}, u32[]{:S(2)}, u32[]{:S(2)}) collective-permute-start(bf16[192,1152]{1,0:T(8,128)(2,1)S(1)} %get-tuple-element.76), channel_id=1, source_target_pairs={{0,1},{1,0},{2,3},{3,2},{4,5},{5,4},{6,7},{7,6},{8,9},{9,8},{10,11... | collective-permute-start | bytes 1327112 | tf_op jit(solution)/shard_map/ppermute | solution.py:407
  158.4 23.9 %collective-permute-start.52 = (bf16[192,1152]{1,0:T(8,128)(2,1)S(1)}, bf16[192,1152]{1,0:T(8,128)(2,1)S(1)}, u32[]{:S(2)}, u32[]{:S(2)}) collective-permute-start(bf16[192,1152]{1,0:T(8,128)(2,1)S(1)} %get-tuple-element.77), channel_id=1, source_target_pairs={{0,8},{1,9},{2,10},{3,11},{4,12},{5,13},{6,14},{7,15},{8,0},{9,1},... | collective-permute-start | bytes 1327112 | tf_op jit(solution)/shard_map/ppermute | solution.py:407
  164.1 26.1 %collective-permute-start.53 = (bf16[192,1152]{1,0:T(8,128)(2,1)S(1)}, bf16[192,1152]{1,0:T(8,128)(2,1)S(1)}, u32[]{:S(2)}, u32[]{:S(2)}) collective-permute-start(bf16[192,1152]{1,0:T(8,128)(2,1)S(1)} %get-tuple-element.78), channel_id=1, source_target_pairs={{0,9},{1,8},{2,11},{3,10},{4,13},{5,12},{6,15},{7,14},{8,1},{9,0},... | collective-permute-start | bytes 1327112 | tf_op jit(solution)/shard_map/ppermute | solution.py:407
  195.5 22.1 %collective-permute-start.57 = (bf16[192,1152]{1,0:T(8,128)(2,1)S(1)}, bf16[192,1152]{1,0:T(8,128)(2,1)S(1)}, u32[]{:S(2)}, u32[]{:S(2)}) collective-permute-start(bf16[192,1152]{1,0:T(8,128)(2,1)S(1)} %last.1.refs_1_), channel_id=1, source_target_pairs={{0,2},{1,3},{2,0},{3,1},{4,6},{5,7},{6,4},{7,5},{8,10},{9,11},{10,... | collective-permute-start | bytes 1327112 | tf_op jit(solution)/shard_map/ppermute | solution.py:399
  197.5 20.1 %collective-permute-start.59 = (bf16[192,1152]{1,0:T(8,128)(2,1)S(1)}, bf16[192,1152]{1,0:T(8,128)(2,1)S(1)}, u32[]{:S(2)}, u32[]{:S(2)}) collective-permute-start(bf16[192,1152]{1,0:T(8,128)(2,1)S(1)} %last.1.refs_1_), channel_id=1, source_target_pairs={{0,1},{1,0},{2,3},{3,2},{4,5},{5,4},{6,7},{7,6},{8,9},{9,8},{10,11... | collective-permute-start | bytes 1327112 | tf_op jit(solution)/shard_map/ppermute | solution.py:399
  242.4 18.5 %collective-permute-start.65 = (bf16[144,1152]{1,0:T(8,128)(2,1)S(1)}, bf16[144,1152]{1,0:T(8,128)(2,1)S(1)}, u32[]{:S(2)}, u32[]{:S(2)}) collective-permute-start(bf16[144,1152]{1,0:T(8,128)(2,1)S(1)} %get-tuple-element.96), channel_id=1, source_target_pairs={{0,8},{4,12},{8,0},{12,4},{16,24},{20,28},{24,16},{28,20},{1,9},{5... | collective-permute-start | bytes 995336 | tf_op jit(solution)/shard_map/ppermute | solution.py:395
  245.1 16.7 %collective-permute-start.67 = (bf16[144,1152]{1,0:T(8,128)(2,1)S(1)}, bf16[144,1152]{1,0:T(8,128)(2,1)S(1)}, u32[]{:S(2)}, u32[]{:S(2)}) collective-permute-start(bf16[144,1152]{1,0:T(8,128)(2,1)S(1)} %get-tuple-element.97), channel_id=1, source_target_pairs={{0,24},{4,28},{8,16},{12,20},{16,8},{20,12},{24,0},{28,4},{1,25},{... | collective-permute-start | bytes 995336 | tf_op jit(solution)/shard_map/ppermute | solution.py:395
  245.6 16.9 %collective-permute-start.66 = (bf16[144,1152]{1,0:T(8,128)(2,1)S(1)}, bf16[144,1152]{1,0:T(8,128)(2,1)S(1)}, u32[]{:S(2)}, u32[]{:S(2)}) collective-permute-start(bf16[144,1152]{1,0:T(8,128)(2,1)S(1)} %get-tuple-element.98), channel_id=1, source_target_pairs={{0,16},{4,20},{8,24},{12,28},{16,0},{20,4},{24,8},{28,12},{1,17},{... | collective-permute-start | bytes 995336 | tf_op jit(solution)/shard_map/ppermute | solution.py:395
  247.5 27.2 %collective-permute-start.62 = (bf16[144,1152]{1,0:T(8,128)(2,1)S(1)}, bf16[144,1152]{1,0:T(8,128)(2,1)S(1)}, u32[]{:S(2)}, u32[]{:S(2)}) collective-permute-start(bf16[144,1152]{1,0:T(8,128)(2,1)S(1)} %get-tuple-element.99), channel_id=1, source_target_pairs={{0,8},{4,12},{8,0},{12,4},{16,24},{20,28},{24,16},{28,20},{1,9},{5... | collective-permute-start | bytes 995336 | tf_op jit(solution)/shard_map/ppermute | solution.py:395
  250.3 24.5 %collective-permute-start.64 = (bf16[144,1152]{1,0:T(8,128)(2,1)S(1)}, bf16[144,1152]{1,0:T(8,128)(2,1)S(1)}, u32[]{:S(2)}, u32[]{:S(2)}) collective-permute-start(bf16[144,1152]{1,0:T(8,128)(2,1)S(1)} %get-tuple-element.100), channel_id=1, source_target_pairs={{0,24},{4,28},{8,16},{12,20},{16,8},{20,12},{24,0},{28,4},{1,25},{... | collective-permute-start | bytes 995336 | tf_op jit(solution)/shard_map/ppermute | solution.py:395
  260.9 15.3 %collective-permute-start.63 = (bf16[144,1152]{1,0:T(8,128)(2,1)S(1)}, bf16[144,1152]{1,0:T(8,128)(2,1)S(1)}, u32[]{:S(2)}, u32[]{:S(2)}) collective-permute-start(bf16[144,1152]{1,0:T(8,128)(2,1)S(1)} %get-tuple-element.101), channel_id=1, source_target_pairs={{0,16},{4,20},{8,24},{12,28},{16,0},{20,4},{24,8},{28,12},{1,17},{... | collective-permute-start | bytes 995336 | tf_op jit(solution)/shard_map/ppermute | solution.py:395
  (64 other events, 838.5 us)

commit v2 on v1

--- a/solution.py
+++ b/solution.py
@@ -115,9 +115,9 @@
             base = dot(upright(state[group, sample]), patch[...], ((1,), (0,)))
             base = place(base, down_pos[group], across[...])
             normed, _ = layer_norm(base)
-            spot = sample * 9 + first_mod
+            spot = sample * (mods.shape[0] // samples) + first_mod
             if per_set:
-                abroad = samples * 9 + sample * 4 + first_mod // 3 * 2
+                abroad = spot - first_mod + 9 + first_mod // 3 * 2
                 spot = jnp.where(group < per_set, spot, abroad)
             shift = mods[pl.ds(spot, 1), :]
             scale = mods[pl.ds(spot + 1, 1), :]
@@ -192,7 +192,7 @@
     mixed = parts[0][rows].astype(F32)
     for part in parts[1:]:
         mixed = mixed + part[rows].astype(F32)
-    gate_row = sample * 9 + gate_at
+    gate_row = sample * (mods.shape[0] // state.shape[0]) + gate_at
     gate = mods[gate_row : gate_row + 1, :]
     base = dot(upright(state[sample]), patch[...], ((1,), (0,)))
     base = place(base, down_pos[0], across[...])
@@ -463,25 +463,25 @@
 
 def modulation_sum(part, samples, fast, square, plane):
     if not fast:
-        return lax.psum_scatter(part, PLANE, scatter_dimension=0, tiled=True)[None]
+        return lax.psum_scatter(part, PLANE, scatter_dimension=0, tiled=True)
     part = part.reshape(plane // 2, 2, samples, part.shape[1])
     pair = part[:, 0] + swap_plane(part[:, 1], 1, plane)
-    sets = 2 if square else 1
-    own = jnp.stack([pair[other] for other in range(sets)], axis=0)
+    share = part.shape[3] // 9
+
+    def sent(flip):
+        if not square:
+            return pair[flip]
+        near = pair[flip ^ 1]
+        return jnp.concatenate([pair[flip], near[:, : 2 * share], near[:, 3 * share : 5 * share]], axis=1)
+
+    own = sent(0)
     for flip in range(1, plane // 2):
-        sent = jnp.stack([pair[flip ^ other] for other in range(sets)], axis=0)
-        own = own + swap_plane(sent, 2 * flip, plane)
+        own = own + swap_plane(sent(flip), 2 * flip, plane)
     return own
 
 
-def modulation_columns(own, columns, col):
-    sets, samples = own.shape[:2]
-    share = own.shape[2] // 9
-    rows = own.reshape(sets, samples, 9, share)
-    packed = [rows[0].reshape(samples * 9, share)]
-    for other in range(1, sets):
-        packed.append(jnp.concatenate([rows[other, :, 0:2], rows[other, :, 3:5]], axis=1).reshape(samples * 4, share))
-    packed = jnp.concatenate(packed, axis=0)
+def modulation_columns(own, share, columns, col):
+    packed = own.reshape(-1, share)
     gathered = spread_col(packed, columns)
     ordered = []
     for place_at in range(columns):
@@ -562,7 +562,7 @@
         labels, step_index, class_table, teacher_mod, student_mod, up_sent, fast, plane
     )
     own_mods = modulation_sum(part, samples, fast, square, plane)
-    mods = modulation_columns(own_mods, columns, col)
+    mods = modulation_columns(own_mods, teacher_mod.shape[2], columns, col)
     teacher_up_pieces = cores(up_shards)
     down_shards = chips(*teacher_shards(teacher_down, down_abroad))
     teacher_down_pieces = cores(down_shards)

time: 278 us -> 277 us (level)
  starting transfers between devices: 70.7 us -> 67.3 us
    ppermute x8, waiting for transfers between devices: 29.2 us -> 34 us  [swap_col(): lax.ppermute(value, 'col', [(spot, spot ^ flip) for spot in range(size)])]
    ppermute x48, waiting for transfers between devices: 54.4 us -> 49.8 us  [swap_plane(): lax.ppermute(value, PLANE, [(spot, spot ^ flip) for spot in range(size)])]
    ppermute x48, starting transfers between devices: 43.6 us -> 39.4 us  [swap_plane(): lax.ppermute(value, PLANE, [(spot, spot ^ flip) for spot in range(size)])]
    unnamed x58 -> x64, local copies, waits for them, and re-layouts: 5.09 us -> 5.67 us
  transfers between devices with their start and end apart: 68 -> 68, of which waited for: 29 -> 32; matrix products, arithmetic and copies ran while one was open for 7% -> 8% of each run, Pallas kernels for 16% -> 16%
where the time goes in v2:
time: 277 us; the launch traced here: 276 us
  waiting for transfers between devices  122 us (44%)
  starting transfers between devices  67.3 us (24%)
  Pallas kernels  59.1 us (21%)
  other arithmetic  13.6 us (5%)
  local copies, waits for them, and re-layouts  11.2 us (4%)
    ppermute x48, waiting for transfers between devices, swap_plane(): lax.ppermute(value, PLANE, [(spot, spot ^ flip) for spot in range(size)])  49.8 us
    ppermute x48, starting transfers between devices, swap_plane(): lax.ppermute(value, PLANE, [(spot, spot ^ flip) for spot in range(size)])  39.4 us
    ppermute x12, waiting for transfers between devices, swap_both(): return lax.ppermute(value, ('dp', 'row', 'col'), pairs)  38.4 us
    ppermute x8, waiting for transfers between devices, swap_col(): lax.ppermute(value, 'col', [(spot, spot ^ flip) for spot in range(size)])  34 us
    pallas_call x3, Pallas kernels, forward(): pl.pallas_call(functools.partial(forward_kernel, count, first_mod, save,...  33.2 us
    ppermute x12, starting transfers between devices, swap_both(): return lax.ppermute(value, ('dp', 'row', 'col'), pairs)  14 us
    ppermute x8, starting transfers between devices, swap_col(): lax.ppermute(value, 'col', [(spot, spot ^ flip) for spot in range(size)])  13.9 us
    pallas_call x3, Pallas kernels, weight_grad(): pl.pallas_call(functools.partial(weight_grad_kernel, len(lefts), len(righ...  11.4 us
  transfers between devices with their start and end apart: 68, of which 32 were waited for; matrix products, arithmetic and copies ran while one was open for 8% of the time, Pallas kernels for 16%

profile of v2, /device:TPU:0, one launch (start us, length us, event | category | flops | bytes accessed | tf_op | source)
XLA Modules:
  0.0 276.4 jit_solution(4056602631964659436)
XLA Ops:
  1.5 3.4 %collective-permute-start.6 = (s32[3]{0:T(128)S(1)}, s32[3]{0:T(128)S(1)}, u32[]{:S(2)}, u32[]{:S(2)}) collective-permute-start(s32[3]{0:T(128)S(1)} %multiply_add_fusion.1), channel_id=1, source_target_pairs={{0,28},{4,24},{8,20},{12,16},{16,12},{20,8},{24,4},{28,0},{1,29},{... | collective-permute-start | bytes 44 | tf_op jit(solution)/shard_map/ppermute | solution.py:395
  7.2 2.8 %collective-permute-start.7 = (bf16[144,1152]{1,0:T(8,128)(2,1)}, bf16[144,1152]{1,0:T(8,128)(2,1)}, u32[]{:S(2)}, u32[]{:S(2)}) collective-permute-start(bf16[144,1152]{1,0:T(8,128)(2,1)} %param.22), channel_id=1, source_target_pairs={{0,2},{1,3},{2,0},{3,1},{4,6},{5,7},{6,4},{7,5},{8,10},{9,11},{10,... | collective-permute-start | bytes 995336 | tf_op jit(solution)/shard_map/ppermute | solution.py:399
  21.7 3.6 %collective-permute-done.7 = bf16[144,1152]{1,0:T(8,128)(2,1)} collective-permute-done((bf16[144,1152]{1,0:T(8,128)(2,1)}, bf16[144,1152]{1,0:T(8,128)(2,1)}, u32[]{:S(2)}, u32[]{:S(2)}) %collective-permute-start.7) | collective-permute-done | bytes 331808 | tf_op jit(solution)/shard_map/ppermute | solution.py:399
  36.3 2.4 collective-permute-start.17
  47.3 3.5 %collective-permute-start.12 = (f32[39,288]{1,0:T(8,128)S(1)}, f32[39,288]{1,0:T(8,128)S(1)}, u32[]{:S(2)}, u32[]{:S(2)}) collective-permute-start(f32[39,288]{1,0:T(8,128)S(1)} %reshape.157), channel_id=1, source_target_pairs={{0,3},{1,2},{2,1},{3,0},{4,7},{5,6},{6,5},{7,4},{8,11},{9,10},{10,... | collective-permute-start | bytes 134792 | tf_op jit(solution)/shard_map/ppermute | solution.py:399
  53.6 6.8 %collective-permute-done.13 = f32[39,288]{1,0:T(8,128)S(1)} collective-permute-done((f32[39,288]{1,0:T(8,128)S(1)}, f32[39,288]{1,0:T(8,128)S(1)}, u32[]{:S(2)}, u32[]{:S(2)}) %collective-permute-start.13) | collective-permute-done | bytes 44960 | tf_op jit(solution)/shard_map/ppermute | solution.py:399
  64.9 2.2 collective-permute-start.21
  69.0 2.2 collective-permute-done.33.refs_10_
  73.2 5.0 %collective-permute-done.28.refs_20_.refs_11_.refs_9_ = bf16[144,1152]{1,0:T(8,128)(2,1)S(1)} collective-permute-done((bf16[144,1152]{1,0:T(8,128)(2,1)S(1)}, bf16[144,1152]{1,0:T(8,128)(2,1)S(1)}, u32[]{:S(2)}, u32[]{:S(2)}) %collective-permute-start.28) | collective-permute-done | bytes 331808 | tf_op jit(solution)/shard_map/ppermute | solution.py:395
  80.2 5.3 %collective-permute-done.21.refs_20_ = bf16[144,1152]{1,0:T(8,128)(2,1)} collective-permute-done((bf16[144,1152]{1,0:T(8,128)(2,1)}, bf16[144,1152]{1,0:T(8,128)(2,1)}, u32[]{:S(2)}, u32[]{:S(2)}) %collective-permute-start.21) | collective-permute-done | bytes 331808 | tf_op jit(solution)/shard_map/ppermute | solution.py:395
  85.4 4.7 %collective-permute-done.19.refs_16_ = bf16[144,1152]{1,0:T(8,128)(2,1)} collective-permute-done((bf16[144,1152]{1,0:T(8,128)(2,1)}, bf16[144,1152]{1,0:T(8,128)(2,1)}, u32[]{:S(2)}, u32[]{:S(2)}) %collective-permute-start.19) | collective-permute-done | bytes 331808 | tf_op jit(solution)/shard_map/ppermute | solution.py:395
  98.0 10.7 %shard_map.158 = (bf16[192,1152]{1,0:T(8,128)(2,1)S(1)}, bf16[192,1152]{1,0:T(8,128)(2,1)S(1)}, bf16[192,1152]{1,0:T(8,128)(2,1)S(1)}, bf16[192,1152]{1,0:T(8,128)(2,1)S(1)}) custom-call(s32[8]{0:T(128)S(1)} %xor_multiply_fusion.refs_0_, f32[4,3,16,64]{3,2,1,0:T(8,128)S(1)} %pad_maximum_fusion.refs_1_, bf16[16,1152]{1,0:T(8,128)(2,1)S(1)} %copy-done.13, ...), custom_call_target="tpu_custom_call" | custom-call | flops 4076863488 | bytes 10616832 | tf_op jit(solution)/shard_map/pallas_call | solution.py:176
  114.8 11.8 %shard_map.159 = (bf16[192,1152]{1,0:T(8,128)(2,1)S(1)}, bf16[192,1152]{1,0:T(8,128)(2,1)S(1)}, bf16[192,1152]{1,0:T(8,128)(2,1)S(1)}, bf16[192,1152]{1,0:T(8,12...) custom-call(s32[8]{0:T(128)S(1)} %xor_multiply_fusion.refs_0_, ...), custom_call_target="tpu_custom_call" | custom-call | flops 4076863488 | bytes 10616832 | tf_op jit(solution)/shard_map/pallas_call | solution.py:176
  126.7 6.2 %collective-permute-done.46.refs_9_ = bf16[192,1152]{1,0:T(8,128)(2,1)S(1)} collective-permute-done((bf16[192,1152]{1,0:T(8,128)(2,1)S(1)}, bf16[192,1152]{1,0:T(8,128)(2,1)S(1)}, u32[]{:S(2)}, u32[]{:S(2)}) %collective-permute-start.46) | collective-permute-done | bytes 442400 | tf_op jit(solution)/shard_map/ppermute | solution.py:407
  138.6 2.5 collective-permute-start.54
  142.7 2.7 collective-permute-start.56
  145.4 10.7 %shard_map.160 = (bf16[192,1152]{1,0:T(8,128)(2,1)S(1)}, bf16[192,1152]{1,0:T(8,128)(2,1)S(1)}, bf16[192,1152]{1,0:T(8,128)(2,1)S(1)}, bf16[192,1152]{1,0:T(8,128)(2,1)S(1)}) custom-call(s32[8]{0:T(128)S(1)} %xor_multiply_fusion.refs_0_, f32[4,3,16,64]{3,2,1,0:T(8,128)S(1)} %pad_maximum_fusion.1.refs_1_, bf16[16,1152]{1,0:T(8,128)(2,1)S(1)} %copy-done.13, ...), custom_call_target="tpu_custom_call" | custom-call | flops 4076863488 | bytes 10616832 | tf_op jit(solution)/shard_map/pallas_call | solution.py:176
  157.3 5.2 %collective-permute-done.54.refs_15_ = bf16[192,1152]{1,0:T(8,128)(2,1)S(1)} collective-permute-done((bf16[192,1152]{1,0:T(8,128)(2,1)S(1)}, bf16[192,1152]{1,0:T(8,128)(2,1)S(1)}, u32[]{:S(2)}, u32[]{:S(2)}) %collective-permute-start.54) | collective-permute-done | bytes 442400 | tf_op jit(solution)/shard_map/ppermute | solution.py:407
  162.5 7.6 %collective-permute-done.55.refs_16_ = bf16[192,1152]{1,0:T(8,128)(2,1)S(1)} collective-permute-done((bf16[192,1152]{1,0:T(8,128)(2,1)S(1)}, bf16[192,1152]{1,0:T(8,128)(2,1)S(1)}, u32[]{:S(2)}, u32[]{:S(2)}) %collective-permute-start.55) | collective-permute-done | bytes 442400 | tf_op jit(solution)/shard_map/ppermute | solution.py:407
  172.2 8.4 %collective-permute-done.51.refs_11_ = bf16[192,1152]{1,0:T(8,128)(2,1)S(1)} collective-permute-done((bf16[192,1152]{1,0:T(8,128)(2,1)S(1)}, bf16[192,1152]{1,0:T(8,128)(2,1)S(1)}, u32[]{:S(2)}, u32[]{:S(2)}) %collective-permute-start.51) | collective-permute-done | bytes 442400 | tf_op jit(solution)/shard_map/ppermute | solution.py:407
  180.6 8.3 %collective-permute-done.53.refs_13_ = bf16[192,1152]{1,0:T(8,128)(2,1)S(1)} collective-permute-done((bf16[192,1152]{1,0:T(8,128)(2,1)S(1)}, bf16[192,1152]{1,0:T(8,128)(2,1)S(1)}, u32[]{:S(2)}, u32[]{:S(2)}) %collective-permute-start.53) | collective-permute-done | bytes 442400 | tf_op jit(solution)/shard_map/ppermute | solution.py:407
  188.9 5.3 %last.1.refs_1_ = bf16[192,1152]{1,0:T(8,128)(2,1)S(1)} custom-call(f32[3,9]{1,0:T(4,128)S(1)} %select_select_fusion.4.refs_0_, f32[3,16,64]{2,1,0:T(8,128)S(1)} %slice_bitcast_fusion.14.refs_1_, f32[3,16,64]{2,1,0:T(8,128)S(1)} %middle.1.refs_2_, bf16[16,1152]{1,0:T(8,128)(2,1)S(1)} %copy-done.13, bf16[16,1152]{1,0:T(8,128)(2,1)S(1)} %copy-done.12, ...), custom_call_target="tpu_custom_call" | custom-call | flops 2000000000 | bytes 4000000 | tf_op jit(solution)/shard_map/last/pallas_call | solution.py:268
  195.4 2.4 collective-permute-start.59
  197.8 18.9 %collective-permute-done.57.refs_3_ = bf16[192,1152]{1,0:T(8,128)(2,1)S(1)} collective-permute-done((bf16[192,1152]{1,0:T(8,128)(2,1)S(1)}, bf16[192,1152]{1,0:T(8,128)(2,1)S(1)}, u32[]{:S(2)}, u32[]{:S(2)}) %collective-permute-start.57) | collective-permute-done | bytes 442400 | tf_op jit(solution)/shard_map/ppermute | solution.py:399
  216.8 4.3 %shard_map.161.refs_2_ = bf16[576,1152]{1,0:T(8,128)(2,1)S(1)} custom-call(s32[8]{0:T(128)S(1)} %xor_multiply_fusion.refs_0_, bf16[192,1152]{1,0:T(8,128)(2,1)S(1)} %last.1.refs_1_, bf16[192,1152]{1,0:T(8,128)(2,1)S(1)} %collective-permute-done.59.refs_2_, bf16[192,1152]{1,0:T(8,128)(2,1)S(1)} %collective-permute-done.57.refs_3_, ...), custom_call_target="tpu_custom_call" | custom-call | flops 1528823808 | bytes 10616832 | tf_op jit(solution)/shard_map/pallas_call | solution.py:373
  221.0 3.1 %shard_map.162.refs_3_ = f32[1152,1152]{1,0:T(8,128)S(1)} custom-call(s32[8]{0:T(128)S(1)} %xor_multiply_fusion.refs_0_, bf16[192,1152]{1,0:T(8,128)(2,1)S(1)} %last.1.refs_1_, bf16[192,1152]{1,0:T(8,128)(2,1)S(1)} %collective-permute-done.59.refs_2_, bf16[192,1152]{1,0:T(8,128)(2,1)S(1)} %collective-permute-done.57.refs_3_, ...), custom_call_target="tpu_custom_call" | custom-call | flops 1528823808 | bytes 10616832 | tf_op jit(solution)/shard_map/pallas_call | solution.py:350
  224.1 4.5 %collective-permute-done.58.refs_1_ = bf16[192,1152]{1,0:T(8,128)(2,1)S(1)} collective-permute-done((bf16[192,1152]{1,0:T(8,128)(2,1)S(1)}, bf16[192,1152]{1,0:T(8,128)(2,1)S(1)}, u32[]{:S(2)}, u32[]{:S(2)}) %collective-permute-start.58) | collective-permute-done | bytes 442400 | tf_op jit(solution)/shard_map/ppermute | solution.py:399
  228.7 3.4 %shard_map.163 = (f32[4,144,1152]{2,1,0:T(8,128)S(1)}, f32[4,144,1152]{2,1,0:T(8,128)S(1)}) custom-call(s32[8]{0:T(128)S(1)} %xor_multiply_fusion.refs_0_, bf16[192,1152]{1,0:T(8,128)(2,1)S(1)} %collective-permute-done.58.refs_1_, bf16[768,1152]{1,0:T(8,128)(2,1)S(1)} %get-tuple-element.70.refs_4_.refs_2_, f32[1152,1152]{1,0:T(8,128)S(1)} %shard_map.162.refs_3_), custom_call_target="tpu_custom_call" | custom-call | flops 509607936 | bytes 10616832 | tf_op jit(solution)/shard_map/pallas_call | solution.py:350
  232.1 2.8 %shard_map.164.refs_3_ = bf16[192,1152]{1,0:T(8,128)(2,1)S(1)} custom-call(s32[8]{0:T(128)S(1)} %xor_multiply_fusion.refs_0_, bf16[192,1152]{1,0:T(8,128)(2,1)S(1)} %collective-permute-done.58.refs_1_, f32[768,1152]{1,0:T(8,128)S(1)} %get-tuple-element.85.refs_4_.refs_2_, bf16[144,1152]{1,0:T(8,128)(2,1)S(1)} %copy-done.2, ...), custom_call_target="tpu_custom_call" | custom-call | flops 509607936 | bytes 10616832 | tf_op jit(solution)/shard_map/pallas_call | solution.py:373
  237.4 5.0 %shard_map.165 = (f32[4,144,1152]{2,1,0:T(8,128)S(1)}, f32[4,144,1152]{2,1,0:T(8,128)S(1)}) custom-call(s32[8]{0:T(128)S(1)} %xor_multiply_fusion.refs_0_, bf16[768,1152]{1,0:T(8,128)(2,1)S(1)} %get-tuple-element.84.refs_1_, bf16[576,1152]{1,0:T(8,128)(2,1)S(1)} %shard_map.161.refs_2_, bf16[192,1152]{1,0:T(8,128)(2,1)S(1)} %shard_map.164.refs_3_), custom_call_target="tpu_custom_call" | custom-call | flops 2038431744 | bytes 10616832 | tf_op jit(solution)/shard_map/pallas_call | solution.py:350
  250.2 10.4 %collective-permute-done.65 = bf16[144,1152]{1,0:T(8,128)(2,1)S(1)} collective-permute-done((bf16[144,1152]{1,0:T(8,128)(2,1)S(1)}, bf16[144,1152]{1,0:T(8,128)(2,1)S(1)}, u32[]{:S(2)}, u32[]{:S(2)}) %collective-permute-start.65) | collective-permute-done | bytes 331808 | tf_op jit(solution)/shard_map/ppermute | solution.py:395
  263.0 11.1 %collective-permute-done.62 = bf16[144,1152]{1,0:T(8,128)(2,1)S(1)} collective-permute-done((bf16[144,1152]{1,0:T(8,128)(2,1)S(1)}, bf16[144,1152]{1,0:T(8,128)(2,1)S(1)}, u32[]{:S(2)}, u32[]{:S(2)}) %collective-permute-start.62) | collective-permute-done | bytes 331808 | tf_op jit(solution)/shard_map/ppermute | solution.py:395
  (249 shorter events, 88.0 us)
Async XLA Ops:
  1.5 15.2 %collective-permute-start.6 = (s32[3]{0:T(128)S(1)}, s32[3]{0:T(128)S(1)}, u32[]{:S(2)}, u32[]{:S(2)}) collective-permute-start(s32[3]{0:T(128)S(1)} %multiply_add_fusion.1), channel_id=1, source_target_pairs={{0,28},{4,24},{8,20},{12,16},{16,12},{20,8},{24,4},{28,0},{1,29},{... | collective-permute-start | bytes 44 | tf_op jit(solution)/shard_map/ppermute | solution.py:395
  7.2 18.1 %collective-permute-start.7 = (bf16[144,1152]{1,0:T(8,128)(2,1)}, bf16[144,1152]{1,0:T(8,128)(2,1)}, u32[]{:S(2)}, u32[]{:S(2)}) collective-permute-start(bf16[144,1152]{1,0:T(8,128)(2,1)} %param.22), channel_id=1, source_target_pairs={{0,2},{1,3},{2,0},{3,1},{4,6},{5,7},{6,4},{7,5},{8,10},{9,11},{10,... | collective-permute-start | bytes 995336 | tf_op jit(solution)/shard_map/ppermute | solution.py:399
  18.6 23.2 %collective-permute-start.16 = (bf16[144,1152]{1,0:T(8,128)(2,1)S(1)}, bf16[144,1152]{1,0:T(8,128)(2,1)S(1)}, u32[]{:S(2)}, u32[]{:S(2)}) collective-permute-start(bf16[144,1152]{1,0:T(8,128)(2,1)S(1)} %copy-done.3), channel_id=1, source_target_pairs={{0,16},{4,20},{8,24},{12,28},{16,0},{20,4},{24,8},{28,12},{1,17},{... | collective-permute-start | bytes 995336 | tf_op jit(solution)/shard_map/ppermute | solution.py:395
  20.1 23.8 %collective-permute-start.15 = (bf16[144,1152]{1,0:T(8,128)(2,1)S(1)}, bf16[144,1152]{1,0:T(8,128)(2,1)}, u32[]{:S(2)}, u32[]{:S(2)}) collective-permute-start(bf16[144,1152]{1,0:T(8,128)(2,1)S(1)} %copy-done.3), channel_id=1, source_target_pairs={{0,8},{4,12},{8,0},{12,4},{16,24},{20,28},{24,16},{28,20},{1,9},{5... | collective-permute-start | bytes 995336 | tf_op jit(solution)/shard_map/ppermute | solution.py:395
  39.0 22.8 %collective-permute-start.18 = (bf16[144,1152]{1,0:T(8,128)(2,1)}, bf16[144,1152]{1,0:T(8,128)(2,1)}, u32[]{:S(2)}, u32[]{:S(2)}) collective-permute-start(bf16[144,1152]{1,0:T(8,128)(2,1)} %param.23), channel_id=1, source_target_pairs={{0,2},{1,3},{2,0},{3,1},{4,6},{5,7},{6,4},{7,5},{8,10},{9,11},{10,... | collective-permute-start | bytes 995336 | tf_op jit(solution)/shard_map/ppermute | solution.py:399
  43.9 16.5 %collective-permute-start.13 = (f32[39,288]{1,0:T(8,128)S(1)}, f32[39,288]{1,0:T(8,128)S(1)}, u32[]{:S(2)}, u32[]{:S(2)}) collective-permute-start(f32[39,288]{1,0:T(8,128)S(1)} %reshape.157), channel_id=1, source_target_pairs={{0,2},{1,3},{2,0},{3,1},{4,6},{5,7},{6,4},{7,5},{8,10},{9,11},{10,... | collective-permute-start | bytes 134792 | tf_op jit(solution)/shard_map/ppermute | solution.py:399
  47.3 14.4 %collective-permute-start.12 = (f32[39,288]{1,0:T(8,128)S(1)}, f32[39,288]{1,0:T(8,128)S(1)}, u32[]{:S(2)}, u32[]{:S(2)}) collective-permute-start(f32[39,288]{1,0:T(8,128)S(1)} %reshape.157), channel_id=1, source_target_pairs={{0,3},{1,2},{2,1},{3,0},{4,7},{5,6},{6,5},{7,4},{8,11},{9,10},{10,... | collective-permute-start | bytes 134792 | tf_op jit(solution)/shard_map/ppermute | solution.py:399
  52.4 16.5 %collective-permute-start.31 = (bf16[144,1152]{1,0:T(8,128)(2,1)}, bf16[144,1152]{1,0:T(8,128)(2,1)S(1)}, u32[]{:S(2)}, u32[]{:S(2)}) collective-permute-start(bf16[144,1152]{1,0:T(8,128)(2,1)} %get-tuple-element.104), channel_id=1, source_target_pairs={{0,8},{4,12},{8,0},{12,4},{16,24},{20,28},{24,16},{28,20},{1,9},{5... | collective-permute-start | bytes 995336 | tf_op jit(solution)/shard_map/ppermute | solution.py:395
  62.4 15.9 %collective-permute-start.28 = (bf16[144,1152]{1,0:T(8,128)(2,1)S(1)}, bf16[144,1152]{1,0:T(8,128)(2,1)S(1)}, u32[]{:S(2)}, u32[]{:S(2)}) collective-permute-start(bf16[144,1152]{1,0:T(8,128)(2,1)S(1)} %copy-done.2), channel_id=1, source_target_pairs={{0,24},{4,28},{8,16},{12,20},{16,8},{20,12},{24,0},{28,4},{1,25},{... | collective-permute-start | bytes 995336 | tf_op jit(solution)/shard_map/ppermute | solution.py:395
  64.9 20.5 %collective-permute-start.21 = (bf16[144,1152]{1,0:T(8,128)(2,1)}, bf16[144,1152]{1,0:T(8,128)(2,1)}, u32[]{:S(2)}, u32[]{:S(2)}) collective-permute-start(bf16[144,1152]{1,0:T(8,128)(2,1)} %get-tuple-element.102), channel_id=1, source_target_pairs={{0,24},{4,28},{8,16},{12,20},{16,8},{20,12},{24,0},{28,4},{1,25},{... | collective-permute-start | bytes 995336 | tf_op jit(solution)/shard_map/ppermute | solution.py:395
  69.0 21.1 %collective-permute-start.19 = (bf16[144,1152]{1,0:T(8,128)(2,1)}, bf16[144,1152]{1,0:T(8,128)(2,1)}, u32[]{:S(2)}, u32[]{:S(2)}) collective-permute-start(bf16[144,1152]{1,0:T(8,128)(2,1)} %get-tuple-element.102), channel_id=1, source_target_pairs={{0,8},{4,12},{8,0},{12,4},{16,24},{20,28},{24,16},{28,20},{1,9},{5... | collective-permute-start | bytes 995336 | tf_op jit(solution)/shard_map/ppermute | solution.py:395
  71.2 19.0 %collective-permute-start.20 = (bf16[144,1152]{1,0:T(8,128)(2,1)S(1)}, bf16[144,1152]{1,0:T(8,128)(2,1)}, u32[]{:S(2)}, u32[]{:S(2)}) collective-permute-start(bf16[144,1152]{1,0:T(8,128)(2,1)S(1)} %get-tuple-element.103.refs_14_), channel_id=1, source_target_pairs={{0,16},{4,20},{8,24},{12,28},{16,0},{20,4},{24,8},{28,12},{1,17},{... | collective-permute-start | bytes 995336 | tf_op jit(solution)/shard_map/ppermute | solution.py:395
  78.7 15.6 %collective-permute-start.37 = (bf16[144,1152]{1,0:T(8,128)(2,1)S(1)}, bf16[144,1152]{1,0:T(8,128)(2,1)}, u32[]{:S(2)}, u32[]{:S(2)}) collective-permute-start(bf16[144,1152]{1,0:T(8,128)(2,1)S(1)} %get-tuple-element.103.refs_14_), channel_id=1, source_target_pairs={{0,4},{4,0},{8,12},{12,8},{16,20},{20,16},{24,28},{28,24},{1,5},{5... | collective-permute-start | bytes 995336 | tf_op jit(solution)/shard_map/ppermute | solution.py:395
  93.3 15.4 %collective-permute-start.27 = (bf16[144,1152]{1,0:T(8,128)(2,1)S(1)}, bf16[144,1152]{1,0:T(8,128)(2,1)S(1)}, u32[]{:S(2)}, u32[]{:S(2)}) collective-permute-start(bf16[144,1152]{1,0:T(8,128)(2,1)S(1)} %copy-done.2), channel_id=1, source_target_pairs={{0,16},{4,20},{8,24},{12,28},{16,0},{20,4},{24,8},{28,12},{1,17},{... | collective-permute-start | bytes 995336 | tf_op jit(solution)/shard_map/ppermute | solution.py:395
  94.3 14.9 %collective-permute-start.26 = (bf16[144,1152]{1,0:T(8,128)(2,1)S(1)}, bf16[144,1152]{1,0:T(8,128)(2,1)S(1)}, u32[]{:S(2)}, u32[]{:S(2)}) collective-permute-start(bf16[144,1152]{1,0:T(8,128)(2,1)S(1)} %copy-done.2), channel_id=1, source_target_pairs={{0,8},{4,12},{8,0},{12,4},{16,24},{20,28},{24,16},{28,20},{1,9},{5... | collective-permute-start | bytes 995336 | tf_op jit(solution)/shard_map/ppermute | solution.py:395
  110.5 16.2 %collective-permute-start.45 = (bf16[192,1152]{1,0:T(8,128)(2,1)S(1)}, bf16[192,1152]{1,0:T(8,128)(2,1)S(1)}, u32[]{:S(2)}, u32[]{:S(2)}) collective-permute-start(bf16[192,1152]{1,0:T(8,128)(2,1)S(1)} %get-tuple-element.57), channel_id=1, source_target_pairs={{0,1},{1,0},{2,3},{3,2},{4,5},{5,4},{6,7},{7,6},{8,9},{9,8},{10,11... | collective-permute-start | bytes 1327112 | tf_op jit(solution)/shard_map/ppermute | solution.py:407
  111.0 21.9 %collective-permute-start.46 = (bf16[192,1152]{1,0:T(8,128)(2,1)S(1)}, bf16[192,1152]{1,0:T(8,128)(2,1)S(1)}, u32[]{:S(2)}, u32[]{:S(2)}) collective-permute-start(bf16[192,1152]{1,0:T(8,128)(2,1)S(1)} %get-tuple-element.58), channel_id=1, source_target_pairs={{0,8},{1,9},{2,10},{3,11},{4,12},{5,13},{6,14},{7,15},{8,0},{9,1},... | collective-permute-start | bytes 1327112 | tf_op jit(solution)/shard_map/ppermute | solution.py:407
  111.8 21.1 %collective-permute-start.47 = (bf16[192,1152]{1,0:T(8,128)(2,1)S(1)}, bf16[192,1152]{1,0:T(8,128)(2,1)S(1)}, u32[]{:S(2)}, u32[]{:S(2)}) collective-permute-start(bf16[192,1152]{1,0:T(8,128)(2,1)S(1)} %get-tuple-element.59), channel_id=1, source_target_pairs={{0,9},{1,8},{2,11},{3,10},{4,13},{5,12},{6,15},{7,14},{8,1},{9,0},... | collective-permute-start | bytes 1327112 | tf_op jit(solution)/shard_map/ppermute | solution.py:407
  138.6 23.9 %collective-permute-start.54 = (bf16[192,1152]{1,0:T(8,128)(2,1)S(1)}, bf16[192,1152]{1,0:T(8,128)(2,1)S(1)}, u32[]{:S(2)}, u32[]{:S(2)}) collective-permute-start(bf16[192,1152]{1,0:T(8,128)(2,1)S(1)} %get-tuple-element.67), channel_id=1, source_target_pairs={{0,2},{1,3},{2,0},{3,1},{4,6},{5,7},{6,4},{7,5},{8,10},{9,11},{10,... | collective-permute-start | bytes 1327112 | tf_op jit(solution)/shard_map/ppermute | solution.py:407
  141.7 28.4 %collective-permute-start.55 = (bf16[192,1152]{1,0:T(8,128)(2,1)S(1)}, bf16[192,1152]{1,0:T(8,128)(2,1)S(1)}, u32[]{:S(2)}, u32[]{:S(2)}) collective-permute-start(bf16[192,1152]{1,0:T(8,128)(2,1)S(1)} %get-tuple-element.79), channel_id=1, source_target_pairs={{0,1},{1,0},{2,3},{3,2},{4,5},{5,4},{6,7},{7,6},{8,9},{9,8},{10,11... | collective-permute-start | bytes 1327112 | tf_op jit(solution)/shard_map/ppermute | solution.py:407
  142.7 29.5 %collective-permute-start.56 = (bf16[192,1152]{1,0:T(8,128)(2,1)S(1)}, bf16[192,1152]{1,0:T(8,128)(2,1)S(1)}, u32[]{:S(2)}, u32[]{:S(2)}) collective-permute-start(bf16[192,1152]{1,0:T(8,128)(2,1)S(1)} %get-tuple-element.80), channel_id=1, source_target_pairs={{0,3},{1,2},{2,1},{3,0},{4,7},{5,6},{6,5},{7,4},{8,11},{9,10},{10,... | collective-permute-start | bytes 1327112 | tf_op jit(solution)/shard_map/ppermute | solution.py:407
  156.2 24.5 %collective-permute-start.51 = (bf16[192,1152]{1,0:T(8,128)(2,1)S(1)}, bf16[192,1152]{1,0:T(8,128)(2,1)S(1)}, u32[]{:S(2)}, u32[]{:S(2)}) collective-permute-start(bf16[192,1152]{1,0:T(8,128)(2,1)S(1)} %get-tuple-element.76), channel_id=1, source_target_pairs={{0,1},{1,0},{2,3},{3,2},{4,5},{5,4},{6,7},{7,6},{8,9},{9,8},{10,11... | collective-permute-start | bytes 1327112 | tf_op jit(solution)/shard_map/ppermute | solution.py:407
  156.5 24.1 %collective-permute-start.52 = (bf16[192,1152]{1,0:T(8,128)(2,1)S(1)}, bf16[192,1152]{1,0:T(8,128)(2,1)S(1)}, u32[]{:S(2)}, u32[]{:S(2)}) collective-permute-start(bf16[192,1152]{1,0:T(8,128)(2,1)S(1)} %get-tuple-element.77), channel_id=1, source_target_pairs={{0,8},{1,9},{2,10},{3,11},{4,12},{5,13},{6,14},{7,15},{8,0},{9,1},... | collective-permute-start | bytes 1327112 | tf_op jit(solution)/shard_map/ppermute | solution.py:407
  162.5 26.4 %collective-permute-start.53 = (bf16[192,1152]{1,0:T(8,128)(2,1)S(1)}, bf16[192,1152]{1,0:T(8,128)(2,1)S(1)}, u32[]{:S(2)}, u32[]{:S(2)}) collective-permute-start(bf16[192,1152]{1,0:T(8,128)(2,1)S(1)} %get-tuple-element.78), channel_id=1, source_target_pairs={{0,9},{1,8},{2,11},{3,10},{4,13},{5,12},{6,15},{7,14},{8,1},{9,0},... | collective-permute-start | bytes 1327112 | tf_op jit(solution)/shard_map/ppermute | solution.py:407
  194.2 22.5 %collective-permute-start.57 = (bf16[192,1152]{1,0:T(8,128)(2,1)S(1)}, bf16[192,1152]{1,0:T(8,128)(2,1)S(1)}, u32[]{:S(2)}, u32[]{:S(2)}) collective-permute-start(bf16[192,1152]{1,0:T(8,128)(2,1)S(1)} %last.1.refs_1_), channel_id=1, source_target_pairs={{0,2},{1,3},{2,0},{3,1},{4,6},{5,7},{6,4},{7,5},{8,10},{9,11},{10,... | collective-permute-start | bytes 1327112 | tf_op jit(solution)/shard_map/ppermute | solution.py:399
  195.4 21.4 %collective-permute-start.59 = (bf16[192,1152]{1,0:T(8,128)(2,1)S(1)}, bf16[192,1152]{1,0:T(8,128)(2,1)S(1)}, u32[]{:S(2)}, u32[]{:S(2)}) collective-permute-start(bf16[192,1152]{1,0:T(8,128)(2,1)S(1)} %last.1.refs_1_), channel_id=1, source_target_pairs={{0,1},{1,0},{2,3},{3,2},{4,5},{5,4},{6,7},{7,6},{8,9},{9,8},{10,11... | collective-permute-start | bytes 1327112 | tf_op jit(solution)/shard_map/ppermute | solution.py:399
  242.7 17.9 %collective-permute-start.65 = (bf16[144,1152]{1,0:T(8,128)(2,1)S(1)}, bf16[144,1152]{1,0:T(8,128)(2,1)S(1)}, u32[]{:S(2)}, u32[]{:S(2)}) collective-permute-start(bf16[144,1152]{1,0:T(8,128)(2,1)S(1)} %get-tuple-element.96), channel_id=1, source_target_pairs={{0,8},{4,12},{8,0},{12,4},{16,24},{20,28},{24,16},{28,20},{1,9},{5... | collective-permute-start | bytes 995336 | tf_op jit(solution)/shard_map/ppermute | solution.py:395
  243.4 18.2 %collective-permute-start.67 = (bf16[144,1152]{1,0:T(8,128)(2,1)S(1)}, bf16[144,1152]{1,0:T(8,128)(2,1)S(1)}, u32[]{:S(2)}, u32[]{:S(2)}) collective-permute-start(bf16[144,1152]{1,0:T(8,128)(2,1)S(1)} %get-tuple-element.97), channel_id=1, source_target_pairs={{0,24},{4,28},{8,16},{12,20},{16,8},{20,12},{24,0},{28,4},{1,25},{... | collective-permute-start | bytes 995336 | tf_op jit(solution)/shard_map/ppermute | solution.py:395
  245.0 17.0 %collective-permute-start.66 = (bf16[144,1152]{1,0:T(8,128)(2,1)S(1)}, bf16[144,1152]{1,0:T(8,128)(2,1)S(1)}, u32[]{:S(2)}, u32[]{:S(2)}) collective-permute-start(bf16[144,1152]{1,0:T(8,128)(2,1)S(1)} %get-tuple-element.98), channel_id=1, source_target_pairs={{0,16},{4,20},{8,24},{12,28},{16,0},{20,4},{24,8},{28,12},{1,17},{... | collective-permute-start | bytes 995336 | tf_op jit(solution)/shard_map/ppermute | solution.py:395
  247.9 26.3 %collective-permute-start.62 = (bf16[144,1152]{1,0:T(8,128)(2,1)S(1)}, bf16[144,1152]{1,0:T(8,128)(2,1)S(1)}, u32[]{:S(2)}, u32[]{:S(2)}) collective-permute-start(bf16[144,1152]{1,0:T(8,128)(2,1)S(1)} %get-tuple-element.99), channel_id=1, source_target_pairs={{0,8},{4,12},{8,0},{12,4},{16,24},{20,28},{24,16},{28,20},{1,9},{5... | collective-permute-start | bytes 995336 | tf_op jit(solution)/shard_map/ppermute | solution.py:395
  248.6 25.5 %collective-permute-start.64 = (bf16[144,1152]{1,0:T(8,128)(2,1)S(1)}, bf16[144,1152]{1,0:T(8,128)(2,1)S(1)}, u32[]{:S(2)}, u32[]{:S(2)}) collective-permute-start(bf16[144,1152]{1,0:T(8,128)(2,1)S(1)} %get-tuple-element.100), channel_id=1, source_target_pairs={{0,24},{4,28},{8,16},{12,20},{16,8},{20,12},{24,0},{28,4},{1,25},{... | collective-permute-start | bytes 995336 | tf_op jit(solution)/shard_map/ppermute | solution.py:395
  260.6 14.8 %collective-permute-start.63 = (bf16[144,1152]{1,0:T(8,128)(2,1)S(1)}, bf16[144,1152]{1,0:T(8,128)(2,1)S(1)}, u32[]{:S(2)}, u32[]{:S(2)}) collective-permute-start(bf16[144,1152]{1,0:T(8,128)(2,1)S(1)} %get-tuple-element.101), channel_id=1, source_target_pairs={{0,16},{4,20},{8,24},{12,28},{16,0},{20,4},{24,8},{28,12},{1,17},{... | collective-permute-start | bytes 995336 | tf_op jit(solution)/shard_map/ppermute | solution.py:395
  (67 other events, 857.0 us)
